TPU v7x, 256 devices: a whole 4x4x8 slice. The times are simulated.
256 devices in a mesh: users: 64 (over z, y, x_hi), cols: 4 (over x_lo, core).
Axes of the slice: x: 4 (x_hi: 2, x_lo: 2; x = x_hi * 2 + x_lo), y: 4, z: 8, core: 2. Of those that a mesh axis runs over, the one named last changes fastest.
Arguments:
- item_ids: int32 [1024, 256], P('users'), may hold values from 0 to 131071, as said below
- lengths: int32 [1024], P('users'), may hold values from 1 to 256, 163840 in all
- seed_rows: int32 [1024, 256], P('users'), may hold values from 0 to 63
- item_table: bfloat16 [131072, 1024], P('users', 'cols'), may hold values from -0.59765625 to 0.59765625
- bilinear: bfloat16 [1024, 1024], P(None, 'cols'), may hold values from -0.1875 to 0.1875
- seed_table: float32 [64, 8], replicated, may hold values from -260 to 260
Outputs:
- capsules: float32 [1024, 8, 1024], P('users', None, 'cols')
Inputs may be any that keep to these rules, and one draw needn't show every extreme that they name: `item_ids`: ids 2048 * s to 2048 * (s + 1) - 1 form table shard s. Of the 4096 ids of one index of users, at most 128 lie in one shard, and exactly 128 lie in some shard.
All inputs are finite; a program needn't handle non-finite values. No bound on the sum of `lengths` on one device may be relied on, other than what follows from the above.
Results may differ from a plain program's by a relative error of at most 0.0046.
Values may be sent and summed in bfloat16 or wider, within the bound.
A program may use at most 128 MiB of HBM per device.

v0:
```python
import jax
import jax.numpy as jnp
from jax import lax
from jax.sharding import PartitionSpec as P

ITERS = 3


def items_in_groups(value, axis, split_dim, concat_dim, work, item_dim, out_dim):

    def moved(group):
        return lax.all_to_all(group, axis, split_axis=split_dim, concat_axis=concat_dim, tiled=True)

    items = jax.tree.leaves(value)[0].shape[item_dim]
    ends = [items * k // 2 for k in range(2 + 1)] if items % 2 == 0 else [0, items]
    groups = [
        jax.tree.map(lambda a: lax.slice_in_dim(a, low, high, axis=item_dim), value)
        for low, high in zip(ends, ends[1:])
    ]
    arrived = [moved(group) for group in groups]
    made = [work(group) for group in arrived]
    return jax.tree.map(lambda *parts: jnp.concatenate(parts, axis=out_dim), *made)


def sent_to_all(value, axis):
    copies = jnp.broadcast_to(value, (lax.axis_size(axis), *value.shape))
    return lax.all_to_all(copies, axis, split_axis=0, concat_axis=0, tiled=True)


def taken_together(value, axis):
    everything = sent_to_all(value, axis)
    return jnp.sum(everything, axis=0)


def squash_scale(squares):
    return squares / (1.0 + squares) / jnp.sqrt(squares + 1e-06)


def owner_ranks(owner, owners):
    tok_count = owner.shape[0]
    span = min(256, tok_count)
    onehot = (owner[:, None] == jnp.arange(owners, dtype=jnp.int32)[None, :]).astype(jnp.float32)
    blocked = onehot.reshape(tok_count // span, span, owners)
    row_ids = lax.broadcasted_iota(jnp.int32, (span, span), 0)
    col_ids = lax.broadcasted_iota(jnp.int32, (span, span), 1)
    lower = (row_ids >= col_ids).astype(jnp.float32)
    within = jnp.einsum("ij,bjo->bio", lower, blocked)
    totals = within[:, -1, :]
    before = jnp.cumsum(totals, axis=0) - totals
    counts = (within + before[:, None, :]).reshape(tok_count, owners)
    return (jnp.sum(counts * onehot, axis=1) - 1.0).astype(jnp.int32)


def on_device(item_ids, lengths, seed_rows, item_table, bilinear, seed_table):
    users_here, hist = item_ids.shape
    owners = lax.axis_size("users")
    rows_dev = item_table.shape[0]
    half = bilinear.shape[1]
    tok_count = users_here * hist
    capacity = max(2, (2 * tok_count + owners - 1) // owners)
    flat_ids = item_ids.reshape(tok_count)
    owner = flat_ids // rows_dev
    row_in = flat_ids % rows_dev
    slot = owner * capacity + owner_ranks(owner, owners)
    requests = (
        jnp.zeros((owners * capacity,), jnp.int32).at[slot].set(row_in).reshape(owners, capacity)
    )
    whole_table = lax.all_gather(item_table, "cols", axis=1, tiled=True)

    def serve(received):
        fetched = whole_table[received.reshape(-1)]
        mapped_rows = jnp.dot(fetched, bilinear, preferred_element_type=jnp.float32).astype(
            jnp.bfloat16
        )
        mapped_rows = mapped_rows.reshape(received.shape + (half,))
        return lax.all_to_all(mapped_rows, "users", split_axis=0, concat_axis=0, tiled=True)

    answers = items_in_groups(requests, "users", 0, 0, serve, 1, 1)
    mapped = answers.reshape(owners * capacity, half)[slot]
    mapped = mapped.reshape(users_here, hist, half)
    seeds = seed_table.shape[0]
    seed_onehot = (
        seed_rows.reshape(tok_count)[:, None] == jnp.arange(seeds, dtype=jnp.int32)[None, :]
    ).astype(jnp.float32)
    logits = jnp.dot(seed_onehot, seed_table, precision=lax.Precision.HIGHEST).reshape(
        users_here, hist, -1
    )
    position = jnp.arange(hist, dtype=jnp.int32)
    live = (position[None, :] < lengths[:, None]).astype(jnp.float32)
    capsules = jnp.zeros((users_here, logits.shape[2], half), jnp.float32)
    for step in range(ITERS):
        weights = (jax.nn.softmax(logits, axis=-1) * live[:, :, None]).astype(jnp.bfloat16)
        summed = jnp.einsum("utk,utd->ukd", weights, mapped, preferred_element_type=jnp.float32)
        partial_value = jnp.sum(summed * summed, axis=-1)
        squares = taken_together(partial_value, "cols")
        capsules = summed * squash_scale(squares)[:, :, None]
        if step + 1 < ITERS:
            products = jnp.einsum(
                "utd,ukd->utk",
                mapped,
                capsules,
                preferred_element_type=jnp.float32,
                precision=lax.Precision.HIGHEST,
            )
            logits = logits + taken_together(products, "cols")
    return capsules


def solution(mesh):
    placed = (
        P("users", None),
        P("users"),
        P("users", None),
        P("users", "cols"),
        P(None, "cols"),
        P(),
    )
    return jax.shard_map(
        on_device, mesh=mesh, in_specs=placed, out_specs=P("users", None, "cols"), check_vma=False
    )
```

profile of v0, /device:TPU:1, one launch (start us, length us, event | category | flops | bytes accessed | tf_op | source)
XLA Modules:
  0.0 294.0 jit_solution(2994380274526949796)
XLA Ops:
  6.5 0.7 all-gather.2.cloned.1.call-update
  7.3 0.7 add_select_fusion.1
  8.0 0.4 convolution_bitcast_fusion
  8.4 0.2 slice.18
  8.6 0.2 copy.18
  8.8 0.2 copy.19
  9.1 0.4 subtract_reduce_fusion
  9.5 0.3 select_reduce_fusion
  9.9 0.1 compare_select_fusion.2
  10.0 15.5 %scatter_custom_fusion = s32[8192]{0:T(1024)S(1)} fusion(s32[4096]{0:T(1024)S(1)} %bitcast.72, s32[4096]{0:T(1024)S(1)} %add_select_fusion, s32[]{:T(128)} %constant.38.clone.1), kind=kCustom, calls=%fused_computation.64 | custom fusion | bytes 32772 | tf_op jit(solution)/shard_map/scatter | solution.py:66
  25.5 0.7 fusion.34
  26.2 25.7 %all_to_all.53 = s32[64,1,64]{2,1,0:T(1,128)S(1)} all-to-all(s32[64,1,64]{2,1,0:T(1,128)S(1)} %bitcast.71), channel_id=1, replica_groups=mesh['users'=64,'cols'=4] {'users'}, dimensions={0} | all-to-all | bytes 32768 | tf_op jit(solution)/shard_map/all_to_all | solution.py:12
  52.0 4.6 %all-to-all-start.2 = ((s32[64,1,64]{2,1,0:T(1,128)}), s32[64,1,64]{2,1,0:T(1,128)S(1)}, u32[]{:S(2)}, u32[]{:S(2)}) async-start(s32[64,1,64]{2,1,0:T(1,128)} %bitcast.9), calls=%async_computation.2 | async-start | bytes 65536 | tf_op jit(solution)/shard_map/all_to_all | solution.py:12
  56.6 0.6 broadcast.249
  57.1 0.7 reduce.16
  57.8 0.1 reshape.298
  58.0 5.2 %all-gather.2.cloned.1.call-done = bf16[2048,1024]{1,0:T(8,128)(2,1)} async-done(((bf16[2048,256]{1,0:T(8,128)(2,1)}), bf16[2048,1024]{1,0:T(8,128)(2,1)}) %all-gather.2.cloned.1.call-update) | async-done | bytes 4194320 | tf_op jit(solution)/shard_map/all_gather | solution.py:68
  63.1 23.6 %gather_fusion = bf16[4096,1024]{1,0:T(8,128)(2,1)} fusion(bf16[2048,1024]{1,0:T(8,128)(2,1)} %all-gather.2.cloned.1.call-done, s32[4096]{0:T(1024)S(1)} %broadcast_clamp_fusion.2), kind=kCustom, calls=%fused_computation | custom fusion | bytes 16793600 | tf_op jit(solution)/shard_map/gather | solution.py:71
  86.8 7.1 %convolution_convert_fusion.1 = bf16[4096,256]{1,0:T(8,128)(2,1)} fusion(bf16[4096,1024]{1,0:T(8,128)(2,1)} %gather_fusion, bf16[1024,256]{1,0:T(8,128)(2,1)S(1)} %copy-done), kind=kOutput, calls=%fused_computation.5 | convolution fusion | flops 2148532224 | bytes 11010048 | tf_op jit(solution)/shard_map/dot_general | solution.py:72
  93.8 12.4 %all-to-all-start.1 = ((bf16[64,64,256]{2,1,0:T(8,128)(2,1)}), bf16[64,64,256]{2,1,0:T(8,128)(2,1)S(1)}, u32[]{:S(2)}, u32[]{:S(2)}) async-start(bf16[64,64,256]{2,1,0:T(8,128)(2,1)} %bitcast.64), calls=%async_computation.1 | async-start | bytes 4194304 | tf_op jit(solution)/shard_map/all_to_all | solution.py:76
  106.2 0.7 reduce.15
  107.0 0.1 reshape.300
  107.1 23.6 %gather_fusion.1 = bf16[4096,1024]{1,0:T(8,128)(2,1)} fusion(bf16[2048,1024]{1,0:T(8,128)(2,1)} %all-gather.2.cloned.1.call-done, s32[4096]{0:T(1024)S(1)} %broadcast_clamp_fusion.1), kind=kCustom, calls=%fused_computation.1 | custom fusion | bytes 16793600 | tf_op jit(solution)/shard_map/gather | solution.py:71
  130.7 7.1 %convolution_convert_fusion = bf16[4096,256]{1,0:T(8,128)(2,1)} fusion(bf16[4096,1024]{1,0:T(8,128)(2,1)} %gather_fusion.1, bf16[1024,256]{1,0:T(8,128)(2,1)S(1)} %copy-done), kind=kOutput, calls=%fused_computation.4 | convolution fusion | flops 2148532224 | bytes 11010048 | tf_op jit(solution)/shard_map/dot_general | solution.py:72
  137.8 19.9 %all-to-all-done.1 = bf16[64,64,256]{2,1,0:T(8,128)(2,1)S(1)} async-done(((bf16[64,64,256]{2,1,0:T(8,128)(2,1)}), bf16[64,64,256]{2,1,0:T(8,128)(2,1)S(1)}, u32[]{:S(2)}, u32[]{:S(2)}) %all-to-all-start.1) | async-done | bytes 2097184 | tf_op jit(solution)/shard_map/all_to_all | solution.py:76
  157.7 7.2 %all-to-all-start.3 = ((bf16[64,64,256]{2,1,0:T(8,128)(2,1)}), bf16[64,64,256]{2,1,0:T(8,128)(2,1)}, u32[]{:S(2)}, u32[]{:S(2)}) async-start(bf16[64,64,256]{2,1,0:T(8,128)(2,1)} %bitcast.65), calls=%async_computation.3 | async-start | bytes 4194304 | tf_op jit(solution)/shard_map/all_to_all | solution.py:76
  164.9 1.9 fusion.35
  167.0 48.0 %all-to-all-done.3 = bf16[64,64,256]{2,1,0:T(8,128)(2,1)} async-done(((bf16[64,64,256]{2,1,0:T(8,128)(2,1)}), bf16[64,64,256]{2,1,0:T(8,128)(2,1)}, u32[]{:S(2)}, u32[]{:S(2)}) %all-to-all-start.3) | async-done | bytes 2097184 | tf_op jit(solution)/shard_map/all_to_all | solution.py:76
  215.0 3.9 %pad_maximum_fusion = bf16[64,128,256]{2,1,0:T(8,128)(2,1)} fusion(bf16[64,64,256]{2,1,0:T(8,128)(2,1)} %all-to-all-done.3, bf16[64,64,256]{2,1,0:T(8,128)(2,1)S(1)} %all-to-all-done.1), kind=kLoop, calls=%fused_computation.6 | loop fusion | flops 8388608 | bytes 8388608 | tf_op jit(solution)/shard_map/concatenate | solution.py:22
  218.9 15.7 %gather_fusion.2 = bf16[4096,256]{1,0:T(8,128)(2,1)S(1)} fusion(bf16[8192,256]{1,0:T(8,128)(2,1)} %bitcast.56, s32[4096]{0:T(1024)S(1)} %broadcast_clamp_fusion), kind=kCustom, calls=%fused_computation.2 | custom fusion | bytes 4210688 | tf_op jit(solution)/shard_map/gather | solution.py:79
  234.6 0.5 multiply_reduce_fusion.2
  235.2 0.1 reshape.356
  235.3 8.2 %all_to_all.54 = f32[4,1,128]{2,1,0:T(1,128)S(1)} all-to-all(f32[4,1,128]{2,1,0:T(1,128)S(1)} %reshape.356), channel_id=1, replica_groups=mesh['users'=64,'cols'=4] {'cols'}, dimensions={0} | all-to-all | bytes 4096 | tf_op jit(solution)/shard_map/all_to_all | solution.py:27
  243.5 0.5 broadcast.251
  244.0 0.7 reduce.17
  244.8 1.7 fusion.7
  246.6 10.9 %all_to_all.55 = f32[4,16,256,8]{2,3,1,0:T(8,128)S(1)} all-to-all(f32[4,16,256,8]{2,3,1,0:T(8,128)S(1)} %broadcast_in_dim.14), channel_id=1, replica_groups=mesh['users'=64,'cols'=4] {'cols'}, dimensions={0} | all-to-all | bytes 1048576 | tf_op jit(solution)/shard_map/all_to_all | solution.py:27
  257.7 0.5 multiply_reduce_fusion.1
  258.2 0.1 reshape.358
  258.3 6.5 %all_to_all.56 = f32[4,1,128]{2,1,0:T(1,128)S(1)} all-to-all(f32[4,1,128]{2,1,0:T(1,128)S(1)} %reshape.358), channel_id=1, replica_groups=mesh['users'=64,'cols'=4] {'cols'}, dimensions={0} | all-to-all | bytes 4096 | tf_op jit(solution)/shard_map/all_to_all | solution.py:27
  264.8 0.7 reduce.18
  265.6 1.7 fusion.5
  267.4 10.9 %all_to_all.57 = f32[4,16,256,8]{2,3,1,0:T(8,128)S(1)} all-to-all(f32[4,16,256,8]{2,3,1,0:T(8,128)S(1)} %broadcast_in_dim.16), channel_id=1, replica_groups=mesh['users'=64,'cols'=4] {'cols'}, dimensions={0} | all-to-all | bytes 1048576 | tf_op jit(solution)/shard_map/all_to_all | solution.py:27
  278.5 0.5 multiply_reduce_fusion
  279.0 0.1 reshape.360
  279.1 6.5 %all_to_all.58 = f32[4,1,128]{2,1,0:T(1,128)S(1)} all-to-all(f32[4,1,128]{2,1,0:T(1,128)S(1)} %reshape.360), channel_id=1, replica_groups=mesh['users'=64,'cols'=4] {'cols'}, dimensions={0} | all-to-all | bytes 4096 | tf_op jit(solution)/shard_map/all_to_all | solution.py:27
  285.5 0.7 reduce.19
  286.4 0.8 broadcast_multiply_fusion
  (59 shorter events, 1.5 us)
Async XLA Ops:
  6.5 80.2 %copy-start = (bf16[1024,256]{1,0:T(8,128)(2,1)S(1)}, bf16[1024,256]{1,0:T(8,128)(2,1)}, u32[]{:S(2)}) copy-start(bf16[1024,256]{1,0:T(8,128)(2,1)} %param.10) | copy-start | bytes 1572868
  6.5 56.6 %all-gather.2.cloned.1.call-start = ((), (), s32[]{:S(2)}) async-start(), calls=%async_computation.9 | async-start | bytes 5242880 | tf_op jit(solution)/shard_map/all_gather | solution.py:68
  8.4 1.4 copy-start.1
  52.0 41.9 %all-to-all-start.2 = ((s32[64,1,64]{2,1,0:T(1,128)}), s32[64,1,64]{2,1,0:T(1,128)S(1)}, u32[]{:S(2)}, u32[]{:S(2)}) async-start(s32[64,1,64]{2,1,0:T(1,128)} %bitcast.9), calls=%async_computation.2 | async-start | bytes 65536 | tf_op jit(solution)/shard_map/all_to_all | solution.py:12
  93.8 63.9 %all-to-all-start.1 = ((bf16[64,64,256]{2,1,0:T(8,128)(2,1)}), bf16[64,64,256]{2,1,0:T(8,128)(2,1)S(1)}, u32[]{:S(2)}, u32[]{:S(2)}) async-start(bf16[64,64,256]{2,1,0:T(8,128)(2,1)} %bitcast.64), calls=%async_computation.1 | async-start | bytes 4194304 | tf_op jit(solution)/shard_map/all_to_all | solution.py:76
  157.7 7.2 %copy-start.2 = (s32[16,256]{1,0:T(8,128)S(1)}, s32[16,256]{1,0:T(8,128)}, u32[]{:S(2)}) copy-start(s32[16,256]{1,0:T(8,128)} %param.8) | copy-start | bytes 49156
  157.7 7.2 %copy-start.4 = (f32[64,8]{0,1:T(8,128)S(1)}, f32[64,8]{0,1:T(8,128)}, u32[]{:S(2)}) copy-start(f32[64,8]{0,1:T(8,128)} %param.11) | copy-start | bytes 6148
  157.7 9.3 %copy-start.3 = (s32[16]{0:T(128)S(1)}, s32[16]{0:T(128)}, u32[]{:S(2)}) copy-start(s32[16]{0:T(128)} %param.7) | copy-start | bytes 196
  157.7 57.3 %all-to-all-start.3 = ((bf16[64,64,256]{2,1,0:T(8,128)(2,1)}), bf16[64,64,256]{2,1,0:T(8,128)(2,1)}, u32[]{:S(2)}, u32[]{:S(2)}) async-start(bf16[64,64,256]{2,1,0:T(8,128)(2,1)} %bitcast.65), calls=%async_computation.3 | async-start | bytes 4194304 | tf_op jit(solution)/shard_map/all_to_all | solution.py:76
Sparse Core Ops, SparseCore 0:
  9.1 53.9 all-gather.1
where the time goes:
time: 295 us; the launch traced here: 294 us
  local copies, waits for them, and re-layouts  82.3 us (28%)
  waiting for transfers between devices  73.7 us (25%)
  blocking collectives  68.6 us (23%)
  starting transfers between devices  24.2 us (8%)
  matrix products  21.3 us (7%)
  between operations  13.8 us (5%)
  other arithmetic  10.1 us (3%)
    all_to_all x2, waiting for transfers between devices, serve(): lax.all_to_all(mapped_rows, 'users', split_axis=0, concat_axis=0, tiled=T...  67.8 us
    gather x2, local copies, waits for them, and re-layouts, serve(): fetched = whole_table[received.reshape(-1)]  47.2 us
    all_to_all x5, blocking collectives, sent_to_all(): return lax.all_to_all(copies, axis, split_axis=0, concat_axis=0, tiled=True)  42.9 us
    all_to_all x1, blocking collectives, moved(): lax.all_to_all(group, axis, split_axis=split_dim, concat_axis=concat_dim,...  25.7 us
    all_to_all x2, starting transfers between devices, serve(): lax.all_to_all(mapped_rows, 'users', split_axis=0, concat_axis=0, tiled=T...  19.6 us
    gather x1, local copies, waits for them, and re-layouts, on_device(): mapped = answers.reshape(owners * capacity, half)[slot]  15.7 us
    scatter x1, local copies, waits for them, and re-layouts, on_device(): jnp.zeros((owners * capacity,), jnp.int32).at[slot].set(row_in)  15.5 us
    dot_general x2, matrix products, serve(): jnp.dot(fetched, bilinear, preferred_element_type=jnp.float32)  14.2 us
  transfers between devices with their start and end apart: 4, of which 3 were waited for; matrix products, arithmetic and copies ran while one was open for 29% of the time, Pallas kernels for 0%

commit v1 on v0

v1 whole, which is shorter than its diff:
```python
import functools

import jax
import jax.numpy as jnp
from jax import lax
from jax.experimental import pallas as pl
from jax.experimental.pallas import tpu as pltpu
from jax.sharding import PartitionSpec as P

ITERS = 3
GROUPS = 64
COLS = 4
LANES = 128
BATCH = 8
CHUNKS = 4
MESH = pl.DeviceIdType.MESH
BF16 = jnp.bfloat16
F32 = jnp.float32
NT = (((1,), (1,)), ((), ()))


def squash_scale(squares):
    return squares / (1.0 + squares) / jnp.sqrt(squares + 1e-06)


def split_two(value):
    high = value.astype(BF16)
    low = (value - high.astype(F32)).astype(BF16)
    return high, low


def softmax_rows(logits):
    shifted = jnp.exp(logits - jnp.max(logits, axis=0, keepdims=True))
    return (shifted / jnp.sum(shifted, axis=0, keepdims=True)).astype(BF16)


def kernel(
    cap,
    ids_ref, len_ref, seed_ref, table_ref, map_ref, seed_table_ref,
    out_ref,
    req_out, req_in, users_of, seeds_of, gathered, mapped, send_rows, rows,
    logits, weights, agree_out, agree_in, square_out, square_in,
    req_send, req_recv, tab_send, tab_recv, relay_send, relay_recv,
    row_send, row_recv, cols_send, cols_recv, sq_send, sq_recv,
):
    me = lax.axis_index("users")
    col = lax.axis_index("cols")
    users, hist = ids_ref.shape
    rows_dev = table_ref.shape[0]
    half = table_ref.shape[1]
    capsules = seed_table_ref.shape[1]
    pairs = users * capsules
    tiles = GROUPS * cap // LANES
    per_tile = LANES // cap
    chunk = rows_dev // CHUNKS
    partner = col + 1 - 2 * lax.rem(col, 2)
    cross = lax.rem(col + 2, COLS)
    diagonal = lax.rem(partner + 2, COLS)

    def group_at(step):
        return lax.rem(me + step, GROUPS)

    barrier = pltpu.get_barrier_semaphore()

    @pl.loop(1, GROUPS)
    def _(step):
        pl.semaphore_signal(barrier, inc=1, device_id={"users": group_at(step)}, device_id_type=MESH)

    for other in (partner, cross, diagonal):
        pl.semaphore_signal(barrier, inc=1, device_id={"cols": other}, device_id_type=MESH)

    position = lax.broadcasted_iota(jnp.int32, (1, hist), 1)
    owner_iota = lax.broadcasted_iota(jnp.int32, (GROUPS, hist), 0)
    tile_iota = lax.broadcasted_iota(jnp.int32, (tiles, hist), 0)
    rank_iota = lax.broadcasted_iota(jnp.int32, (LANES, hist), 0)
    upper = (
        lax.broadcasted_iota(jnp.int32, (hist, hist), 0)
        <= lax.broadcasted_iota(jnp.int32, (hist, hist), 1)
    ).astype(F32).astype(BF16)
    ones = jnp.ones((hist, hist), BF16)
    tri = jnp.concatenate([upper, ones], axis=0)
    before = jnp.zeros((GROUPS, hist), F32)
    requests = jnp.zeros((2 * GROUPS, LANES), F32)
    meta = jnp.zeros((2 * tiles, LANES), F32)
    for user in range(users):
        ids = ids_ref[user : user + 1, :]
        owner = ids // rows_dev
        row = ids - owner * rows_dev
        live = position < len_ref[user]
        owner = jnp.where(live, owner, -1)
        onehot = jnp.where(owner_iota == owner, 1.0, 0.0)
        both = jnp.concatenate([onehot.astype(BF16), before.astype(BF16)], axis=1)
        counts = jnp.dot(both, tri, preferred_element_type=F32)
        before = before + onehot
        rank = (jnp.sum(counts * onehot, axis=0, keepdims=True) - 1.0).astype(jnp.int32)
        high = (row // 256).astype(F32) + 8.0
        low = (row - row // 256 * 256).astype(F32)
        left = jnp.concatenate([(onehot * high).astype(BF16), (onehot * low).astype(BF16)], axis=0)
        at_rank = jnp.where(rank_iota == rank, 1.0, 0.0).astype(BF16)
        requests = requests + lax.dot_general(left, at_rank, NT, preferred_element_type=F32)
        tile = jnp.where(rank < cap, owner // per_tile, -1)
        place = rank + (owner - owner // per_tile * per_tile) * cap
        onehot_tile = jnp.where(tile_iota == tile, 1.0, 0.0)
        seeds = seed_ref[user : user + 1, :].astype(F32)
        left = jnp.concatenate(
            [(onehot_tile * (user + 1.0)).astype(BF16), (onehot_tile * seeds).astype(BF16)], axis=0
        )
        at_place = jnp.where(rank_iota == place, 1.0, 0.0).astype(BF16)
        meta = meta + lax.dot_general(left, at_place, NT, preferred_element_type=F32)
    asked = (requests[:GROUPS] - 8.0) * 256.0 + requests[GROUPS:]
    asked = jnp.where(requests[:GROUPS] > 0.0, asked, -1.0).astype(jnp.int32)
    for owner in range(GROUPS):
        req_out[owner] = asked[owner : owner + 1, :]
    user_ids = meta[:tiles].astype(jnp.int32) - 1
    seed_ids = meta[tiles:].astype(jnp.int32)
    for tile in range(tiles):
        users_of[tile] = jnp.broadcast_to(user_ids[tile : tile + 1, :], (8, LANES))
        seeds_of[tile] = jnp.broadcast_to(seed_ids[tile : tile + 1, :], (8, LANES))

    pl.semaphore_wait(barrier, GROUPS - 1 + COLS - 1)

    def table_copy(part, target, slot):
        return pltpu.make_async_remote_copy(
            src_ref=table_ref.at[pl.ds(part * chunk, chunk)],
            dst_ref=gathered.at[col, pl.ds(part * chunk, chunk)],
            send_sem=tab_send.at[slot, part],
            recv_sem=tab_recv.at[slot, part],
            device_id={"cols": target},
            device_id_type=MESH,
        )

    def relay_copy(part):
        return pltpu.make_async_remote_copy(
            src_ref=gathered.at[cross, pl.ds(part * chunk, chunk)],
            dst_ref=gathered.at[cross, pl.ds(part * chunk, chunk)],
            send_sem=relay_send.at[part],
            recv_sem=relay_recv.at[part],
            device_id={"cols": partner},
            device_id_type=MESH,
        )

    for part in range(CHUNKS):
        table_copy(part, cross, 0).start()
    for part in range(CHUNKS):
        table_copy(part, partner, 1).start()

    def request_copy(target, landing):
        return pltpu.make_async_remote_copy(
            src_ref=req_out.at[target],
            dst_ref=req_in.at[landing],
            send_sem=req_send.at[target],
            recv_sem=req_recv.at[landing],
            device_id={"users": target},
            device_id_type=MESH,
        )

    @pl.loop(1, GROUPS)
    def _(step):
        request_copy(group_at(step), me).start()

    req_in[me] = req_out[me]

    seed_table = seed_table_ref[...]
    seed_high, seed_low = split_two(seed_table)
    seed_rest = (seed_table - seed_high.astype(F32) - seed_low.astype(F32)).astype(BF16)
    seed_count = seed_table.shape[0]
    seed_iota = lax.broadcasted_iota(jnp.int32, (seed_count, LANES), 0)

    def store_weights(tile, value):
        picked = users_of[tile]
        routed = softmax_rows(value).astype(F32)
        stacked = jnp.concatenate(
            [jnp.where(picked == user, routed, 0.0) for user in range(users)], axis=0
        )
        weights[tile] = stacked.astype(BF16)

    @pl.loop(0, tiles)
    def _(tile):
        chosen = jnp.where(seed_iota == seeds_of[tile][0:1, :], 1.0, 0.0).astype(BF16)
        start = jnp.zeros((capsules, LANES), F32)
        for part in (seed_rest, seed_low, seed_high):
            start = start + lax.dot_general(
                part, chosen, (((0,), (0,)), ((), ())), preferred_element_type=F32
            )
        logits[tile] = start
        store_weights(tile, start)

    for part in range(CHUNKS):
        table_copy(part, cross, 0).wait_recv()
        relay_copy(part).start()
    for part in range(CHUNKS):
        table_copy(part, partner, 1).wait_recv()
        relay_copy(part).wait_recv()
        span = pl.ds(part * chunk, chunk)
        value = jnp.dot(table_ref[span], map_ref[col], preferred_element_type=F32)
        for source in (partner, cross, diagonal):
            value = value + jnp.dot(gathered[source, span], map_ref[source], preferred_element_type=F32)
        mapped[span] = value.astype(BF16)

    @pl.loop(1, GROUPS)
    def _(step):
        request_copy(group_at(step), group_at(step)).wait_recv()

    def row_copy(target, landing):
        return pltpu.make_async_remote_copy(
            src_ref=send_rows.at[target],
            dst_ref=rows.at[landing],
            send_sem=row_send.at[target],
            recv_sem=row_recv.at[landing],
            device_id={"users": target},
            device_id_type=MESH,
        )

    batches = GROUPS // BATCH
    lane_iota = lax.broadcasted_iota(jnp.int32, (cap, rows_dev), 1)

    @pl.loop(0, batches)
    def _(batch):
        wanted = jnp.concatenate(
            [req_in[group_at(batch + batches * item)] for item in range(BATCH)], axis=0
        )
        columns = wanted.astype(F32).T.astype(jnp.int32)
        onehot = jnp.concatenate(
            [
                jnp.where(lane_iota == columns[:cap, item : item + 1], 1.0, 0.0).astype(BF16)
                for item in range(BATCH)
            ],
            axis=0,
        )
        served = jnp.dot(onehot, mapped[...], preferred_element_type=F32).astype(BF16)
        for item in range(BATCH):
            send_rows[group_at(batch + batches * item)] = served[item * cap : (item + 1) * cap]
        for item in range(BATCH):
            if item:
                row_copy(group_at(batch + batches * item), me).start()
            else:

                @pl.when(batch > 0)
                def _():
                    row_copy(group_at(batch), me).start()

    rows[me] = send_rows[me]

    @pl.loop(1, GROUPS)
    def _(step):
        row_copy(group_at(step), group_at(step)).wait_recv()

    def cols_copy(step, hop, target):
        source = agree_out.at[step] if hop == 0 else agree_out.at[2 + step]
        return pltpu.make_async_remote_copy(
            src_ref=source,
            dst_ref=agree_in.at[2 * step + hop],
            send_sem=cols_send.at[2 * step + hop],
            recv_sem=cols_recv.at[2 * step + hop],
            device_id={"cols": target},
            device_id_type=MESH,
        )

    lane_of = lax.broadcasted_iota(jnp.int32, (8, LANES), 1)
    per_source = cap // LANES if cap > LANES else 1
    del per_source

    def tile_rows(tile):
        if per_tile == 1:
            return rows[tile]
        return jnp.concatenate([rows[tile * per_tile + k] for k in range(per_tile)], axis=0)

    for step in range(ITERS):
        summed = lax.fori_loop(
            0,
            tiles // 2,
            lambda i, acc: acc
            + jnp.dot(
                jnp.concatenate([weights[2 * i], weights[2 * i + 1]], axis=1),
                jnp.concatenate([tile_rows(2 * i), tile_rows(2 * i + 1)], axis=0),
                preferred_element_type=F32,
            ),
            jnp.zeros((pairs, half), F32),
        )
        partial = jnp.sum(summed * summed, axis=1, keepdims=True)
        packed = jnp.zeros((8, LANES), F32)
        for user in range(users):
            packed = jnp.where(lane_of == user, partial[user * 8 : user * 8 + 8], packed)
        if step + 1 < ITERS:
            parts = jnp.concatenate(split_two(summed), axis=0)

            @pl.loop(0, tiles // 2)
            def _(i):
                landed = jnp.concatenate([tile_rows(2 * i), tile_rows(2 * i + 1)], axis=0)
                product = lax.dot_general(parts, landed, NT, preferred_element_type=F32)
                product = product[:pairs] + product[pairs:]
                for k in range(2):
                    picked = users_of[2 * i + k]
                    own = jnp.zeros((8, LANES), F32)
                    for user in range(users):
                        piece = product[user * 8 : user * 8 + 8, k * LANES : (k + 1) * LANES]
                        own = jnp.where(picked == user, piece, own)
                    agree_out[step, 2 * i + k] = own

            agree_out[step, tiles] = packed
            cols_copy(step, 0, partner).start()
            cols_copy(step, 0, partner).wait_recv()
            agree_out[2 + step] = agree_out[step] + agree_in[2 * step]
            cols_copy(step, 1, cross).start()
            cols_copy(step, 1, cross).wait_recv()
            squares = agree_out[2 + step, tiles] + agree_in[2 * step + 1, tiles]
            scale = squash_scale(squares)
            scales = [jnp.broadcast_to(scale[:, user : user + 1], (8, LANES)) for user in range(users)]

            @pl.loop(0, tiles)
            def _(tile):
                picked = users_of[tile]
                factor = jnp.zeros((8, LANES), F32)
                for user in range(users):
                    factor = jnp.where(picked == user, scales[user], factor)
                total = agree_out[2 + step, tile] + agree_in[2 * step + 1, tile]
                value = logits[tile] + factor * total
                logits[tile] = value
                store_weights(tile, value)

        else:
            square_out[...] = packed
            copies = []
            for slot, target in enumerate((partner, cross, diagonal)):
                copies.append(
                    pltpu.make_async_remote_copy(
                        src_ref=square_out,
                        dst_ref=square_in.at[slot],
                        send_sem=sq_send.at[slot],
                        recv_sem=sq_recv.at[slot],
                        device_id={"cols": target},
                        device_id_type=MESH,
                    )
                )
            for copy in copies:
                copy.start()
            for copy in copies:
                copy.wait_recv()
            squares = (square_out[...] + square_in[0]) + (square_in[1] + square_in[2])
            scale = squash_scale(squares)
            for user in range(users):
                out_ref[user] = summed[user * 8 : user * 8 + 8] * scale[:, user : user + 1]
            for copy in copies:
                copy.wait_send()

    for part in range(CHUNKS):
        table_copy(part, cross, 0).wait_send()
        table_copy(part, partner, 1).wait_send()
        relay_copy(part).wait_send()

    @pl.loop(1, GROUPS)
    def _(step):
        request_copy(group_at(step), me).wait_send()
        row_copy(group_at(step), me).wait_send()

    for step in range(ITERS - 1):
        cols_copy(step, 0, partner).wait_send()
        cols_copy(step, 1, cross).wait_send()


def on_device(cap, item_ids, lengths, seed_rows, item_table, bilinear, seed_table):
    users, hist = item_ids.shape
    rows_dev, half = item_table.shape
    capsules = seed_table.shape[1]
    tiles = GROUPS * cap // LANES
    vmem = pl.BlockSpec(memory_space=pltpu.VMEM)
    dma = pltpu.SemaphoreType.DMA
    return pl.pallas_call(
        functools.partial(kernel, cap),
        out_shape=jax.ShapeDtypeStruct((users, capsules, half), F32),
        in_specs=[vmem, pl.BlockSpec(memory_space=pltpu.SMEM), vmem, vmem, vmem, vmem],
        out_specs=vmem,
        scratch_shapes=[
            pltpu.VMEM((GROUPS, 1, LANES), jnp.int32),
            pltpu.VMEM((GROUPS, 1, LANES), jnp.int32),
            pltpu.VMEM((tiles, 8, LANES), jnp.int32),
            pltpu.VMEM((tiles, 8, LANES), jnp.int32),
            pltpu.VMEM((COLS, rows_dev, half), BF16),
            pltpu.VMEM((rows_dev, half), BF16),
            pltpu.VMEM((GROUPS, cap, half), BF16),
            pltpu.VMEM((GROUPS, cap, half), BF16),
            pltpu.VMEM((tiles, 8, LANES), F32),
            pltpu.VMEM((tiles, users * capsules, LANES), BF16),
            pltpu.VMEM((4, tiles + 1, 8, LANES), F32),
            pltpu.VMEM((4, tiles + 1, 8, LANES), F32),
            pltpu.VMEM((8, LANES), F32),
            pltpu.VMEM((3, 8, LANES), F32),
            dma((GROUPS,)), dma((GROUPS,)),
            dma((2, CHUNKS)), dma((2, CHUNKS)), dma((CHUNKS,)), dma((CHUNKS,)),
            dma((GROUPS,)), dma((GROUPS,)),
            dma((4,)), dma((4,)), dma((3,)), dma((3,)),
        ],
        compiler_params=pltpu.CompilerParams(
            collective_id=0, has_side_effects=True, vmem_limit_bytes=56 << 20
        ),
    )(item_ids, lengths, seed_rows, item_table, bilinear.reshape(COLS, -1, half), seed_table)


def solution(mesh):
    placed = (
        P("users", None),
        P("users"),
        P("users", None),
        P("users", "cols"),
        P(None, "cols"),
        P(),
    )
    return jax.shard_map(
        functools.partial(on_device, 128),
        mesh=mesh,
        in_specs=placed,
        out_specs=P("users", None, "cols"),
        check_vma=False,
    )
```

time: 295 us -> 200 us (0.68)
  Pallas kernels: 0 us -> 197 us
  local copies, waits for them, and re-layouts: 82.3 us -> 2.95 us
  waiting for transfers between devices: 73.7 us -> 0 us
  blocking collectives: 68.6 us -> 0 us
  starting transfers between devices: 24.2 us -> 0 us
  matrix products: 21.3 us -> 0 us
  between operations: 13.8 us -> 0.01 us
  other arithmetic: 10.1 us -> 0 us
    pallas_call x0 -> x1, Pallas kernels: none -> 197 us  [on_device(): pl.pallas_call(functools.partial(kernel, cap), out_shape=jax.ShapeDtypeSt...]
    all_to_all x6 -> x0, blocking collectives: 68.6 us -> none  [the longest x5 42.9 us: sent_to_all(): return lax.all_to_all(copies, axis, split_axis=0, concat_axis=0, tiled=True)]
    all_to_all x3 -> x0, waiting for transfers between devices: 67.8 us -> none  [the longest x2 67.8 us: serve(): lax.all_to_all(mapped_rows, 'users', split_axis=0, concat_axis=0, tiled=T...]
    gather x3 -> x0, local copies, waits for them, and re-layouts: 63 us -> none  [the longest x2 47.2 us: serve(): fetched = whole_table[received.reshape(-1)]]
    all_to_all x3 -> x0, starting transfers between devices: 24.2 us -> none  [the longest x2 19.6 us: serve(): lax.all_to_all(mapped_rows, 'users', split_axis=0, concat_axis=0, tiled=T...]
    dot_general x9 -> x0, matrix products: 21.3 us -> none  [the longest x2 14.2 us: serve(): jnp.dot(fetched, bilinear, preferred_element_type=jnp.float32)]
    scatter x1 -> x0, local copies, waits for them, and re-layouts: 15.5 us -> none  [on_device(): jnp.zeros((owners * capacity,), jnp.int32).at[slot].set(row_in)]
    all_gather x1 -> x0, waiting for transfers between devices: 5.15 us -> none  [on_device(): whole_table = lax.all_gather(item_table, 'cols', axis=1, tiled=True)]
  transfers between devices with their start and end apart: 4 -> 0, of which waited for: 3 -> 0; matrix products, arithmetic and copies ran while one was open for 29% -> 0% of each run, Pallas kernels for 0% -> 0%
where the time goes in v1:
time: 200 us
  Pallas kernels  197 us (98%)
  local copies, waits for them, and re-layouts  2.95 us (1%)
    pallas_call x1, Pallas kernels, on_device(): pl.pallas_call(functools.partial(kernel, cap), out_shape=jax.ShapeDtypeSt...  197 us

profile of v1, /device:TPU:1, one launch (start us, length us, event | category | flops | bytes accessed | tf_op | source)
XLA Modules:
  0.0 200.1 jit_solution(5341850488229033105)
XLA Ops:
  0.0 1.4 copy.7.seed_table_ref
  1.4 197.1 %shard_map.64 = f32[16,8,256]{2,1,0:T(8,128)} custom-call(s32[16,256]{1,0:T(8,128)} %ids_ref.1, s32[16]{0:T(128)} %len_ref.1, s32[16,256]{1,0:T(8,128)} %seed_ref.1, bf16[2048,256]{1,0:T(8,128)(2,1)} %table_ref.1, bf16[4,256,256]{2,1,0:T(8,128)(2,1)} %bitcast.1, f32[64,8]{1,0:T(8,128)} %copy.7.seed_table_ref), custom_call_target="tpu_custom_call" | custom-call | tf_op jit(solution)/shard_map/pallas_call | solution.py:368
  198.5 1.6 copy.9

commit v2 on v1

--- a/solution.py
+++ b/solution.py
@@ -13,6 +13,8 @@
 LANES = 128
 BATCH = 8
 CHUNKS = 4
+HOP = 8
+SPILL = 2
 MESH = pl.DeviceIdType.MESH
 BF16 = jnp.bfloat16
 F32 = jnp.float32
@@ -37,11 +39,13 @@
 def kernel(
     cap,
     ids_ref, len_ref, seed_ref, table_ref, map_ref, seed_table_ref,
-    out_ref,
+    out_ref, fail_ref,
     req_out, req_in, users_of, seeds_of, gathered, mapped, send_rows, rows,
     logits, weights, agree_out, agree_in, square_out, square_in,
+    ask_out, ask_in, relay_rows_out, relay_rows_in, relay_stage, spill_out, spill_in, spill_stage,
     req_send, req_recv, tab_send, tab_recv, relay_send, relay_recv,
     row_send, row_recv, cols_send, cols_recv, sq_send, sq_recv,
+    ask_send, ask_recv, hop_send, hop_recv, spill_send, spill_recv,
 ):
     me = lax.axis_index("users")
     col = lax.axis_index("cols")
@@ -50,7 +54,9 @@
     half = table_ref.shape[1]
     capsules = seed_table_ref.shape[1]
     pairs = users * capsules
-    tiles = GROUPS * cap // LANES
+    relayed = cap < LANES
+    main_tiles = GROUPS * cap // LANES
+    tiles = main_tiles + (1 if relayed else 0)
     per_tile = LANES // cap
     chunk = rows_dev // CHUNKS
     partner = col + 1 - 2 * lax.rem(col, 2)
@@ -80,35 +86,71 @@
     ones = jnp.ones((hist, hist), BF16)
     tri = jnp.concatenate([upper, ones], axis=0)
     before = jnp.zeros((GROUPS, hist), F32)
-    requests = jnp.zeros((2 * GROUPS, LANES), F32)
-    meta = jnp.zeros((2 * tiles, LANES), F32)
+    owners, in_rows, ranks = [], [], []
     for user in range(users):
         ids = ids_ref[user : user + 1, :]
         owner = ids // rows_dev
-        row = ids - owner * rows_dev
-        live = position < len_ref[user]
-        owner = jnp.where(live, owner, -1)
+        in_rows.append(ids - owner * rows_dev)
+        owner = jnp.where(position < len_ref[user], owner, -1)
+        owners.append(owner)
         onehot = jnp.where(owner_iota == owner, 1.0, 0.0)
         both = jnp.concatenate([onehot.astype(BF16), before.astype(BF16)], axis=1)
         counts = jnp.dot(both, tri, preferred_element_type=F32)
         before = before + onehot
-        rank = (jnp.sum(counts * onehot, axis=0, keepdims=True) - 1.0).astype(jnp.int32)
+        ranks.append((jnp.sum(counts * onehot, axis=0, keepdims=True) - 1.0).astype(jnp.int32))
+    if relayed:
+        over = [jnp.where(rank >= cap, 1.0, 0.0) for rank in ranks]
+        over_rows = jnp.concatenate(over, axis=0)
+        over_before = [jnp.zeros((1, hist), F32)]
+        for user in range(users):
+            over_before.append(over_before[-1] + over[user])
+        sums = jnp.concatenate(over_before[:users], axis=0)
+        both = jnp.concatenate([over_rows.astype(BF16), sums.astype(BF16)], axis=1)
+        queue = (jnp.dot(both, tri, preferred_element_type=F32) - 1.0).astype(jnp.int32)
+        over_total = jnp.sum(over_before[users], axis=1, keepdims=True)
+    requests = jnp.zeros((3 * GROUPS, LANES), F32)
+    meta = jnp.zeros((2 * tiles, LANES), F32)
+    for user in range(users):
+        owner, row, rank = owners[user], in_rows[user], ranks[user]
+        target, place = owner, rank
+        tile = owner // per_tile
+        spot = rank + (owner - tile * per_tile) * cap
+        tile = jnp.where(owner >= 0, tile, -1)
+        if relayed:
+            line = queue[user : user + 1, :]
+            turn = line // GROUPS
+            spills = rank >= cap
+            fits = turn < SPILL
+            relay = lax.rem(line + me * 9, GROUPS)
+            target = jnp.where(spills, jnp.where(fits, relay, -1), owner)
+            place = jnp.where(spills, cap + turn, rank)
+            tile = jnp.where(spills, jnp.where(fits, main_tiles, -1), tile)
+            spot = jnp.where(spills, relay * SPILL + turn, spot)
+        onehot = jnp.where(owner_iota == target, 1.0, 0.0)
         high = (row // 256).astype(F32) + 8.0
         low = (row - row // 256 * 256).astype(F32)
-        left = jnp.concatenate([(onehot * high).astype(BF16), (onehot * low).astype(BF16)], axis=0)
-        at_rank = jnp.where(rank_iota == rank, 1.0, 0.0).astype(BF16)
-        requests = requests + lax.dot_general(left, at_rank, NT, preferred_element_type=F32)
-        tile = jnp.where(rank < cap, owner // per_tile, -1)
-        place = rank + (owner - owner // per_tile * per_tile) * cap
+        left = jnp.concatenate(
+            [(onehot * part).astype(BF16) for part in (high, low, owner.astype(F32))], axis=0
+        )
+        at_place = jnp.where(rank_iota == place, 1.0, 0.0).astype(BF16)
+        requests = requests + lax.dot_general(left, at_place, NT, preferred_element_type=F32)
         onehot_tile = jnp.where(tile_iota == tile, 1.0, 0.0)
         seeds = seed_ref[user : user + 1, :].astype(F32)
         left = jnp.concatenate(
             [(onehot_tile * (user + 1.0)).astype(BF16), (onehot_tile * seeds).astype(BF16)], axis=0
         )
-        at_place = jnp.where(rank_iota == place, 1.0, 0.0).astype(BF16)
-        meta = meta + lax.dot_general(left, at_place, NT, preferred_element_type=F32)
-    asked = (requests[:GROUPS] - 8.0) * 256.0 + requests[GROUPS:]
-    asked = jnp.where(requests[:GROUPS] > 0.0, asked, -1.0).astype(jnp.int32)
+        at_spot = jnp.where(rank_iota == spot, 1.0, 0.0).astype(BF16)
+        meta = meta + lax.dot_general(left, at_spot, NT, preferred_element_type=F32)
+    asked = (requests[:GROUPS] - 8.0) * 256.0 + requests[GROUPS : 2 * GROUPS]
+    lane_all = lax.broadcasted_iota(jnp.int32, (GROUPS, LANES), 1)
+    if relayed:
+        whole = asked + requests[2 * GROUPS :] * float(rows_dev)
+        asked = jnp.where(lane_all < cap, asked, whole)
+    asked = jnp.where(requests[:GROUPS] > 0.0, asked, -1.0)
+    if relayed:
+        too_many = jnp.where(over_total > float(SPILL * GROUPS), 1.0, 0.0)
+        asked = jnp.where(lane_all == LANES - 1, too_many, asked)
+    asked = asked.astype(jnp.int32)
     for owner in range(GROUPS):
         req_out[owner] = asked[owner : owner + 1, :]
     user_ids = meta[:tiles].astype(jnp.int32) - 1
@@ -139,25 +181,37 @@
             device_id_type=MESH,
         )
 
+    def users_copy(source, landing_in, sends, recvs, target, landing):
+        return pltpu.make_async_remote_copy(
+            src_ref=source.at[target],
+            dst_ref=landing_in.at[landing],
+            send_sem=sends.at[target],
+            recv_sem=recvs.at[landing],
+            device_id={"users": target},
+            device_id_type=MESH,
+        )
+
+    request_copy = functools.partial(users_copy, req_out, req_in, req_send, req_recv)
+    row_copy = functools.partial(users_copy, send_rows, rows, row_send, row_recv)
+    ask_copy = functools.partial(users_copy, ask_out, ask_in, ask_send, ask_recv)
+    hop_copy = functools.partial(users_copy, relay_rows_out, relay_rows_in, hop_send, hop_recv)
+    spill_copy = functools.partial(users_copy, spill_out, spill_in, spill_send, spill_recv)
+
+    def send_all(copy):
+        @pl.loop(1, GROUPS)
+        def _(step):
+            copy(group_at(step), me).start()
+
+    def receive_all(copy):
+        @pl.loop(1, GROUPS)
+        def _(step):
+            copy(group_at(step), group_at(step)).wait_recv()
+
+    send_all(request_copy)
     for part in range(CHUNKS):
         table_copy(part, cross, 0).start()
     for part in range(CHUNKS):
         table_copy(part, partner, 1).start()
-
-    def request_copy(target, landing):
-        return pltpu.make_async_remote_copy(
-            src_ref=req_out.at[target],
-            dst_ref=req_in.at[landing],
-            send_sem=req_send.at[target],
-            recv_sem=req_recv.at[landing],
-            device_id={"users": target},
-            device_id_type=MESH,
-        )
-
-    @pl.loop(1, GROUPS)
-    def _(step):
-        request_copy(group_at(step), me).start()
-
     req_in[me] = req_out[me]
 
     seed_table = seed_table_ref[...]
@@ -174,8 +228,16 @@
         )
         weights[tile] = stacked.astype(BF16)
 
-    @pl.loop(0, tiles)
-    def _(tile):
+    def each_tile(body):
+        @pl.loop(0, main_tiles // 4)
+        def _(i):
+            for k in range(4):
+                body(4 * i + k)
+
+        if relayed:
+            body(main_tiles)
+
+    def first_weights(tile):
         chosen = jnp.where(seed_iota == seeds_of[tile][0:1, :], 1.0, 0.0).astype(BF16)
         start = jnp.zeros((capsules, LANES), F32)
         for part in (seed_rest, seed_low, seed_high):
@@ -184,6 +246,45 @@
             )
         logits[tile] = start
         store_weights(tile, start)
+
+    each_tile(first_weights)
+
+    receive_all(request_copy)
+
+    if relayed:
+        tokens = GROUPS * SPILL
+        token_lane = lax.broadcasted_iota(jnp.int32, (GROUPS, tokens), 1)
+        token_row = lax.broadcasted_iota(jnp.int32, (GROUPS, tokens), 0)
+        message = jnp.concatenate([req_in[g] for g in range(GROUPS)], axis=0)
+        wanted = jnp.zeros((GROUPS, tokens), F32)
+        for turn in range(SPILL):
+            column = message[:, cap + turn : cap + turn + 1].astype(F32) + 1.0
+            wanted = jnp.where(token_lane == token_row * SPILL + turn, column, wanted)
+        token = jnp.sum(wanted, axis=0, keepdims=True).astype(jnp.int32) - 1
+        owner = token // rows_dev
+        row = token - owner * rows_dev
+        owner = jnp.where(token >= 0, owner, -1)
+        onehot = jnp.where(token_row == owner, 1.0, 0.0)
+        counts = jnp.dot(onehot.astype(BF16), upper[:tokens, :tokens], preferred_element_type=F32)
+        rank = (jnp.sum(counts * onehot, axis=0, keepdims=True) - 1.0).astype(jnp.int32)
+        high = (row // 256).astype(F32) + 8.0
+        low = (row - row // 256 * 256).astype(F32)
+        left = jnp.concatenate([(onehot * high).astype(BF16), (onehot * low).astype(BF16)], axis=0)
+        at_rank = jnp.where(rank_iota[:, :tokens] == rank, 1.0, 0.0).astype(BF16)
+        hops = lax.dot_general(left, at_rank, NT, preferred_element_type=F32)
+        asked = (hops[:GROUPS] - 8.0) * 256.0 + hops[GROUPS:]
+        asked = jnp.where(hops[:GROUPS] > 0.0, asked, -1.0)
+        flags = jnp.where(lane_all == LANES - 1, message.astype(F32), 0.0)
+        flags = jnp.max(jnp.max(flags, axis=0, keepdims=True), axis=1, keepdims=True)
+        deep = jnp.max(rank.astype(F32), axis=1, keepdims=True)
+        flags = jnp.maximum(flags, jnp.where(deep >= float(HOP), 1.0, 0.0))
+        asked = jnp.where(lane_all == LANES - 1, flags, asked).astype(jnp.int32)
+        for target in range(GROUPS):
+            ask_out[target] = asked[target : target + 1, :]
+        landed_at = jnp.where(owner >= 0, owner * HOP + rank, -1)
+        landed_at = jnp.broadcast_to(landed_at, (8, tokens)).astype(F32).T.astype(jnp.int32)[:, 0:1]
+        send_all(ask_copy)
+        ask_in[me] = ask_out[me]
 
     for part in range(CHUNKS):
         table_copy(part, cross, 0).wait_recv()
@@ -197,25 +298,33 @@
             value = value + jnp.dot(gathered[source, span], map_ref[source], preferred_element_type=F32)
         mapped[span] = value.astype(BF16)
 
-    @pl.loop(1, GROUPS)
-    def _(step):
-        request_copy(group_at(step), group_at(step)).wait_recv()
-
-    def row_copy(target, landing):
-        return pltpu.make_async_remote_copy(
-            src_ref=send_rows.at[target],
-            dst_ref=rows.at[landing],
-            send_sem=row_send.at[target],
-            recv_sem=row_recv.at[landing],
-            device_id={"users": target},
-            device_id_type=MESH,
-        )
+    if relayed:
+        receive_all(ask_copy)
+        message = jnp.concatenate([ask_in[g] for g in range(GROUPS)], axis=0).astype(F32)
+        flags = jnp.where(lane_all == LANES - 1, message, 0.0)
+        flags = jnp.max(jnp.max(flags, axis=0, keepdims=True), axis=1, keepdims=True)
+        fail_ref[...] = jnp.broadcast_to(flags, (8, LANES)).astype(jnp.int32)
+        columns = message.T.astype(jnp.int32)
+        hop_iota = lax.broadcasted_iota(jnp.int32, (HOP, rows_dev), 1)
+        onehot = jnp.concatenate(
+            [
+                jnp.where(hop_iota == columns[:HOP, g : g + 1], 1.0, 0.0)
+                for g in range(GROUPS)
+            ],
+            axis=0,
+        ).astype(BF16)
+        served = jnp.dot(onehot, mapped[...], preferred_element_type=F32)
+        for g in range(GROUPS):
+            relay_rows_out[g] = served[g * HOP : (g + 1) * HOP].astype(BF16)
+        send_all(hop_copy)
+        relay_rows_in[me] = relay_rows_out[me]
+    else:
+        fail_ref[...] = jnp.zeros((8, LANES), jnp.int32)
 
     batches = GROUPS // BATCH
     lane_iota = lax.broadcasted_iota(jnp.int32, (cap, rows_dev), 1)
 
-    @pl.loop(0, batches)
-    def _(batch):
+    def serve(batch):
         wanted = jnp.concatenate(
             [req_in[group_at(batch + batches * item)] for item in range(BATCH)], axis=0
         )
@@ -239,11 +348,34 @@
                 def _():
                     row_copy(group_at(batch), me).start()
 
+    early = batches // 2 if relayed else batches
+
+    @pl.loop(0, early)
+    def _(batch):
+        serve(batch)
+
+    if relayed:
+        receive_all(hop_copy)
+        for g in range(GROUPS):
+            relay_stage[g * HOP : (g + 1) * HOP] = relay_rows_in[g].astype(F32)
+        hop_lane = lax.broadcasted_iota(jnp.int32, (tokens, GROUPS * HOP), 1)
+        onehot = jnp.where(hop_lane == landed_at, 1.0, 0.0).astype(BF16)
+        spilled = jnp.dot(onehot, relay_stage[...].astype(BF16), preferred_element_type=F32)
+        for g in range(GROUPS):
+            spill_out[g] = spilled[g * SPILL : (g + 1) * SPILL].astype(BF16)
+        send_all(spill_copy)
+        spill_in[me] = spill_out[me]
+
+        @pl.loop(early, batches)
+        def _(batch):
+            serve(batch)
+
     rows[me] = send_rows[me]
-
-    @pl.loop(1, GROUPS)
-    def _(step):
-        row_copy(group_at(step), group_at(step)).wait_recv()
+    receive_all(row_copy)
+    if relayed:
+        receive_all(spill_copy)
+        for g in range(GROUPS):
+            spill_stage[g * SPILL : (g + 1) * SPILL] = spill_in[g].astype(F32)
 
     def cols_copy(step, hop, target):
         source = agree_out.at[step] if hop == 0 else agree_out.at[2 + step]
@@ -257,26 +389,26 @@
         )
 
     lane_of = lax.broadcasted_iota(jnp.int32, (8, LANES), 1)
-    per_source = cap // LANES if cap > LANES else 1
-    del per_source
-
-    def tile_rows(tile):
-        if per_tile == 1:
-            return rows[tile]
-        return jnp.concatenate([rows[tile * per_tile + k] for k in range(per_tile)], axis=0)
+    wide = 2 * LANES // cap
+
+    def landed(i):
+        return jnp.concatenate([rows[i * wide + k] for k in range(wide)], axis=0)
+
+    def weigh(i):
+        both = jnp.concatenate([weights[2 * i], weights[2 * i + 1]], axis=1)
+        return jnp.dot(both, landed(i), preferred_element_type=F32)
 
     for step in range(ITERS):
         summed = lax.fori_loop(
             0,
-            tiles // 2,
+            main_tiles // 8,
             lambda i, acc: acc
-            + jnp.dot(
-                jnp.concatenate([weights[2 * i], weights[2 * i + 1]], axis=1),
-                jnp.concatenate([tile_rows(2 * i), tile_rows(2 * i + 1)], axis=0),
-                preferred_element_type=F32,
-            ),
+            + ((weigh(4 * i) + weigh(4 * i + 1)) + (weigh(4 * i + 2) + weigh(4 * i + 3))),
             jnp.zeros((pairs, half), F32),
         )
+        if relayed:
+            spilled = spill_stage[...].astype(BF16)
+            summed = summed + jnp.dot(weights[main_tiles], spilled, preferred_element_type=F32)
         partial = jnp.sum(summed * summed, axis=1, keepdims=True)
         packed = jnp.zeros((8, LANES), F32)
         for user in range(users):
@@ -284,19 +416,24 @@
         if step + 1 < ITERS:
             parts = jnp.concatenate(split_two(summed), axis=0)
 
-            @pl.loop(0, tiles // 2)
-            def _(i):
-                landed = jnp.concatenate([tile_rows(2 * i), tile_rows(2 * i + 1)], axis=0)
-                product = lax.dot_general(parts, landed, NT, preferred_element_type=F32)
+            def agree(tile, count, block):
+                product = lax.dot_general(parts, block, NT, preferred_element_type=F32)
                 product = product[:pairs] + product[pairs:]
-                for k in range(2):
-                    picked = users_of[2 * i + k]
+                for k in range(count):
+                    picked = users_of[tile + k]
                     own = jnp.zeros((8, LANES), F32)
                     for user in range(users):
                         piece = product[user * 8 : user * 8 + 8, k * LANES : (k + 1) * LANES]
                         own = jnp.where(picked == user, piece, own)
-                    agree_out[step, 2 * i + k] = own
-
+                    agree_out[step, tile + k] = own
+
+            @pl.loop(0, main_tiles // 4)
+            def _(i):
+                for k in range(2):
+                    agree(4 * i + 2 * k, 2, landed(2 * i + k))
+
+            if relayed:
+                agree(main_tiles, 1, spilled)
             agree_out[step, tiles] = packed
             cols_copy(step, 0, partner).start()
             cols_copy(step, 0, partner).wait_recv()
@@ -307,8 +444,7 @@
             scale = squash_scale(squares)
             scales = [jnp.broadcast_to(scale[:, user : user + 1], (8, LANES)) for user in range(users)]
 
-            @pl.loop(0, tiles)
-            def _(tile):
+            def next_weights(tile):
                 picked = users_of[tile]
                 factor = jnp.zeros((8, LANES), F32)
                 for user in range(users):
@@ -317,6 +453,8 @@
                 value = logits[tile] + factor * total
                 logits[tile] = value
                 store_weights(tile, value)
+
+            each_tile(next_weights)
 
         else:
             square_out[...] = packed
@@ -352,24 +490,31 @@
     def _(step):
         request_copy(group_at(step), me).wait_send()
         row_copy(group_at(step), me).wait_send()
+        if relayed:
+            ask_copy(group_at(step), me).wait_send()
+            hop_copy(group_at(step), me).wait_send()
+            spill_copy(group_at(step), me).wait_send()
 
     for step in range(ITERS - 1):
         cols_copy(step, 0, partner).wait_send()
         cols_copy(step, 1, cross).wait_send()
 
 
-def on_device(cap, item_ids, lengths, seed_rows, item_table, bilinear, seed_table):
+def routed(cap, collective_id, item_ids, lengths, seed_rows, item_table, bilinear, seed_table):
     users, hist = item_ids.shape
     rows_dev, half = item_table.shape
     capsules = seed_table.shape[1]
-    tiles = GROUPS * cap // LANES
+    tiles = GROUPS * cap // LANES + (1 if cap < LANES else 0)
     vmem = pl.BlockSpec(memory_space=pltpu.VMEM)
     dma = pltpu.SemaphoreType.DMA
     return pl.pallas_call(
         functools.partial(kernel, cap),
-        out_shape=jax.ShapeDtypeStruct((users, capsules, half), F32),
+        out_shape=[
+            jax.ShapeDtypeStruct((users, capsules, half), F32),
+            jax.ShapeDtypeStruct((8, LANES), jnp.int32),
+        ],
         in_specs=[vmem, pl.BlockSpec(memory_space=pltpu.SMEM), vmem, vmem, vmem, vmem],
-        out_specs=vmem,
+        out_specs=[vmem, vmem],
         scratch_shapes=[
             pltpu.VMEM((GROUPS, 1, LANES), jnp.int32),
             pltpu.VMEM((GROUPS, 1, LANES), jnp.int32),
@@ -385,15 +530,32 @@
             pltpu.VMEM((4, tiles + 1, 8, LANES), F32),
             pltpu.VMEM((8, LANES), F32),
             pltpu.VMEM((3, 8, LANES), F32),
+            pltpu.VMEM((GROUPS, 1, LANES), jnp.int32),
+            pltpu.VMEM((GROUPS, 1, LANES), jnp.int32),
+            pltpu.VMEM((GROUPS, HOP, half), BF16),
+            pltpu.VMEM((GROUPS, HOP, half), BF16),
+            pltpu.VMEM((GROUPS * HOP, half), F32),
+            pltpu.VMEM((GROUPS, SPILL, half), BF16),
+            pltpu.VMEM((GROUPS, SPILL, half), BF16),
+            pltpu.VMEM((GROUPS * SPILL, half), F32),
             dma((GROUPS,)), dma((GROUPS,)),
             dma((2, CHUNKS)), dma((2, CHUNKS)), dma((CHUNKS,)), dma((CHUNKS,)),
             dma((GROUPS,)), dma((GROUPS,)),
             dma((4,)), dma((4,)), dma((3,)), dma((3,)),
+            dma((GROUPS,)), dma((GROUPS,)), dma((GROUPS,)), dma((GROUPS,)),
+            dma((GROUPS,)), dma((GROUPS,)),
         ],
         compiler_params=pltpu.CompilerParams(
-            collective_id=0, has_side_effects=True, vmem_limit_bytes=56 << 20
+            collective_id=collective_id, has_side_effects=True, vmem_limit_bytes=56 << 20
         ),
-    )(item_ids, lengths, seed_rows, item_table, bilinear.reshape(COLS, -1, half), seed_table)
+    )(item_ids, lengths, seed_rows, item_table, bilinear, seed_table)
+
+
+def on_device(item_ids, lengths, seed_rows, item_table, bilinear, seed_table):
+    maps = bilinear.reshape(COLS, -1, bilinear.shape[1])
+    args = (item_ids, lengths, seed_rows, item_table, maps, seed_table)
+    fast, fail = routed(64, 0, *args)
+    return lax.cond(fail[0, 0] > 0, lambda: routed(LANES, 1, *args)[0], lambda: fast)
 
 
 def solution(mesh):
@@ -406,9 +568,5 @@
         P(),
     )
     return jax.shard_map(
-        functools.partial(on_device, 128),
-        mesh=mesh,
-        in_specs=placed,
-        out_specs=P("users", None, "cols"),
-        check_vma=False,
+        on_device, mesh=mesh, in_specs=placed, out_specs=P("users", None, "cols"), check_vma=False
     )

time: 200 us -> 136 us (0.68)
  Pallas kernels: 197 us -> 130 us
    pallas_call x1, Pallas kernels: 197 us -> 130 us  [routed(): pl.pallas_call(functools.partial(kernel, cap), out_shape=[jax.ShapeDtypeS...]
where the time goes in v2:
time: 136 us; the launch traced here: 135 us
  Pallas kernels  130 us (96%)
  local copies, waits for them, and re-layouts  3.94 us (3%)
    pallas_call x1, Pallas kernels, routed(): pl.pallas_call(functools.partial(kernel, cap), out_shape=[jax.ShapeDtypeS...  130 us
    unnamed x14, local copies, waits for them, and re-layouts  2.75 us

profile of v2, /device:TPU:1, one launch (start us, length us, event | category | flops | bytes accessed | tf_op | source)
XLA Modules:
  0.0 135.1 jit_solution(10075252643542335735)
XLA Ops:
  0.0 0.0 copy-start
  0.0 1.5 %copy.9.seed_table_ref = f32[64,8]{1,0:T(8,128)} copy(f32[64,8]{0,1:T(8,128)} %param.13) | data formatting | bytes 4096 | tf_op args[5]
  1.5 0.0 copy-start.1
  1.5 0.0 copy-start.2
  1.5 0.0 copy-start.3
  1.5 130.4 %shard_map.66 = (f32[16,8,256]{2,1,0:T(8,128)S(1)}, s32[8,128]{1,0:T(8,128)}) custom-call(s32[16,256]{1,0:T(8,128)} %ids_ref.1, s32[16]{0:T(128)} %len_ref.1, s32[16,256]{1,0:T(8,128)} %seed_ref.1, bf16[2048,256]{1,0:T(8,128)(2,1)} %table_ref.1, bf16[4,256,256]{2,1,0:T(8,128)(2,1)} %bitcast.2, f32[64,8]{1,0:T(8,128)} %copy.9.seed_table_ref), custom_call_target="tpu_custom_call" | custom-call | tf_op jit(solution)/shard_map/pallas_call | solution.py:510
  131.9 0.0 copy-start.4
  131.9 1.2 slice.3
  133.7 0.0 copy-start.5
  133.8 0.0 copy-done
  133.8 0.0 copy-done.1
  133.8 0.0 copy-done.2
  133.8 0.0 copy-done.3
  133.8 0.0 copy-done.4
  133.8 0.6 copy-done.5
  134.4 0.7 copy.14
  (1 shorter events, 0.0 us)
Async XLA Ops:
  0.0 133.8 %copy-start = (bf16[2048,256]{1,0:T(8,128)(2,1)S(1)}, bf16[2048,256]{1,0:T(8,128)(2,1)}, u32[]{:S(2)}) copy-start(bf16[2048,256]{1,0:T(8,128)(2,1)} %table_ref.1) | copy-start | bytes 3145732
  1.5 132.3 %copy-start.1 = (bf16[1024,256]{1,0:T(8,128)(2,1)S(1)}, bf16[1024,256]{1,0:T(8,128)(2,1)}, u32[]{:S(2)}) copy-start(bf16[1024,256]{1,0:T(8,128)(2,1)} %param.12) | copy-start | bytes 1572868
  1.5 132.3 %copy-start.2 = (s32[16,256]{1,0:T(8,128)S(1)}, s32[16,256]{1,0:T(8,128)}, u32[]{:S(2)}) copy-start(s32[16,256]{1,0:T(8,128)} %ids_ref.1) | copy-start | bytes 49156
  1.5 132.3 %copy-start.3 = (s32[16,256]{1,0:T(8,128)S(1)}, s32[16,256]{1,0:T(8,128)}, u32[]{:S(2)}) copy-start(s32[16,256]{1,0:T(8,128)} %seed_ref.1) | copy-start | bytes 49156
  131.9 1.9 %copy-start.4 = (f32[64,8]{0,1:T(8,128)S(1)}, f32[64,8]{0,1:T(8,128)}, u32[]{:S(2)}) copy-start(f32[64,8]{0,1:T(8,128)} %param.13) | copy-start | bytes 6148
  133.7 0.7 copy-start.5

commit v3 on v2

--- a/solution.py
+++ b/solution.py
@@ -13,7 +13,9 @@
 LANES = 128
 BATCH = 8
 CHUNKS = 4
-HOP = 8
+HOP = 4
+EARLY = 16
+SPANS = ((0, 8), (8, 16), (16, 24), (24, 32))
 SPILL = 2
 MESH = pl.DeviceIdType.MESH
 BF16 = jnp.bfloat16
@@ -40,19 +42,19 @@
     cap,
     ids_ref, len_ref, seed_ref, table_ref, map_ref, seed_table_ref,
     out_ref, fail_ref,
-    req_out, req_in, users_of, seeds_of, gathered, mapped, send_rows, rows,
+    req_out, req_in, users_of, seeds_of, gathered, mapped, send_rows, rows, send_early, rows_early,
     logits, weights, agree_out, agree_in, square_out, square_in,
     ask_out, ask_in, relay_rows_out, relay_rows_in, relay_stage, spill_out, spill_in, spill_stage,
     req_send, req_recv, tab_send, tab_recv, relay_send, relay_recv,
     row_send, row_recv, cols_send, cols_recv, sq_send, sq_recv,
-    ask_send, ask_recv, hop_send, hop_recv, spill_send, spill_recv,
+    ask_send, ask_recv, hop_send, hop_recv, spill_send, spill_recv, early_send, early_recv,
 ):
     me = lax.axis_index("users")
     col = lax.axis_index("cols")
     users, hist = ids_ref.shape
     rows_dev = table_ref.shape[0]
     half = table_ref.shape[1]
-    capsules = seed_table_ref.shape[1]
+    capsules = seed_table_ref.shape[0]
     pairs = users * capsules
     relayed = cap < LANES
     main_tiles = GROUPS * cap // LANES
@@ -64,7 +66,8 @@
     diagonal = lax.rem(partner + 2, COLS)
 
     def group_at(step):
-        return lax.rem(me + step, GROUPS)
+        pair = lax.rem(me // 2 + step // 2, GROUPS // 2)
+        return 2 * pair + lax.rem(me + step, 2)
 
     barrier = pltpu.get_barrier_semaphore()
 
@@ -86,6 +89,7 @@
     ones = jnp.ones((hist, hist), BF16)
     tri = jnp.concatenate([upper, ones], axis=0)
     before = jnp.zeros((GROUPS, hist), F32)
+    before_first = jnp.zeros((GROUPS, hist), F32)
     owners, in_rows, ranks = [], [], []
     for user in range(users):
         ids = ids_ref[user : user + 1, :]
@@ -97,7 +101,19 @@
         both = jnp.concatenate([onehot.astype(BF16), before.astype(BF16)], axis=1)
         counts = jnp.dot(both, tri, preferred_element_type=F32)
         before = before + onehot
-        ranks.append((jnp.sum(counts * onehot, axis=0, keepdims=True) - 1.0).astype(jnp.int32))
+        rank = jnp.sum(counts * onehot, axis=0, keepdims=True) - 1.0
+        if relayed:
+            first = in_rows[user] < rows_dev // 2
+            onehot_first = jnp.where(first, onehot, 0.0)
+            both = jnp.concatenate([onehot_first.astype(BF16), before_first.astype(BF16)], axis=1)
+            counts = jnp.dot(both, tri, preferred_element_type=F32)
+            before_first = before_first + onehot_first
+            rank_first = jnp.sum(counts * onehot, axis=0, keepdims=True)
+            kept = jnp.minimum(rank_first, float(EARLY))
+            reserved = jnp.logical_and(first, rank_first <= float(EARLY))
+            rank = jnp.where(reserved, rank_first - 1.0, EARLY + rank - kept)
+            rank = jnp.where(owner >= 0, rank, -1.0)
+        ranks.append(rank.astype(jnp.int32))
     if relayed:
         over = [jnp.where(rank >= cap, 1.0, 0.0) for rank in ranks]
         over_rows = jnp.concatenate(over, axis=0)
@@ -193,6 +209,7 @@
 
     request_copy = functools.partial(users_copy, req_out, req_in, req_send, req_recv)
     row_copy = functools.partial(users_copy, send_rows, rows, row_send, row_recv)
+    early_copy = functools.partial(users_copy, send_early, rows_early, early_send, early_recv)
     ask_copy = functools.partial(users_copy, ask_out, ask_in, ask_send, ask_recv)
     hop_copy = functools.partial(users_copy, relay_rows_out, relay_rows_in, hop_send, hop_recv)
     spill_copy = functools.partial(users_copy, spill_out, spill_in, spill_send, spill_recv)
@@ -202,10 +219,14 @@
         def _(step):
             copy(group_at(step), me).start()
 
+    def source_at(step):
+        pair = lax.rem(me // 2 + GROUPS // 2 - step // 2, GROUPS // 2)
+        return 2 * pair + lax.rem(me + step, 2)
+
     def receive_all(copy):
         @pl.loop(1, GROUPS)
         def _(step):
-            copy(group_at(step), group_at(step)).wait_recv()
+            copy(source_at(step), source_at(step)).wait_recv()
 
     send_all(request_copy)
     for part in range(CHUNKS):
@@ -217,7 +238,7 @@
     seed_table = seed_table_ref[...]
     seed_high, seed_low = split_two(seed_table)
     seed_rest = (seed_table - seed_high.astype(F32) - seed_low.astype(F32)).astype(BF16)
-    seed_count = seed_table.shape[0]
+    seed_count = seed_table.shape[1]
     seed_iota = lax.broadcasted_iota(jnp.int32, (seed_count, LANES), 0)
 
     def store_weights(tile, value):
@@ -241,9 +262,7 @@
         chosen = jnp.where(seed_iota == seeds_of[tile][0:1, :], 1.0, 0.0).astype(BF16)
         start = jnp.zeros((capsules, LANES), F32)
         for part in (seed_rest, seed_low, seed_high):
-            start = start + lax.dot_general(
-                part, chosen, (((0,), (0,)), ((), ())), preferred_element_type=F32
-            )
+            start = start + jnp.dot(part, chosen, preferred_element_type=F32)
         logits[tile] = start
         store_weights(tile, start)
 
@@ -286,24 +305,72 @@
         send_all(ask_copy)
         ask_in[me] = ask_out[me]
 
-    for part in range(CHUNKS):
-        table_copy(part, cross, 0).wait_recv()
-        relay_copy(part).start()
-    for part in range(CHUNKS):
-        table_copy(part, partner, 1).wait_recv()
-        relay_copy(part).wait_recv()
-        span = pl.ds(part * chunk, chunk)
-        value = jnp.dot(table_ref[span], map_ref[col], preferred_element_type=F32)
-        for source in (partner, cross, diagonal):
-            value = value + jnp.dot(gathered[source, span], map_ref[source], preferred_element_type=F32)
-        mapped[span] = value.astype(BF16)
+    batches = GROUPS // BATCH
+    stride = 2 * batches
+
+    def step_of(batch, item):
+        return 2 * batch + stride * (item // 2) + item % 2
+
+    def serve(batch, low, high, shard, out, copy):
+        wanted = jnp.concatenate(
+            [req_in[group_at(step_of(batch, item))] for item in range(BATCH)], axis=0
+        )
+        columns = wanted.astype(F32).T.astype(jnp.int32)
+        size = high - low
+        lane_iota = lax.broadcasted_iota(jnp.int32, (size, shard), 1)
+        onehot = jnp.concatenate(
+            [
+                jnp.where(lane_iota == columns[low:high, item : item + 1], 1.0, 0.0).astype(BF16)
+                for item in range(BATCH)
+            ],
+            axis=0,
+        )
+        served = jnp.dot(onehot, mapped[:shard], preferred_element_type=F32).astype(BF16)
+        for item in range(BATCH):
+            out[group_at(step_of(batch, item))] = served[item * size : (item + 1) * size]
+        for item in range(BATCH):
+            if item:
+                copy(group_at(step_of(batch, item)), me).start()
+            else:
+
+                @pl.when(batch > 0)
+                def _():
+                    copy(group_at(step_of(batch, 0)), me).start()
+
+    def map_parts(parts):
+        for part in parts:
+            table_copy(part, cross, 0).wait_recv()
+            relay_copy(part).start()
+        for part in parts:
+            table_copy(part, partner, 1).wait_recv()
+            relay_copy(part).wait_recv()
+            span = pl.ds(part * chunk, chunk)
+            value = jnp.dot(table_ref[span], map_ref[col], preferred_element_type=F32)
+            for source in (partner, cross, diagonal):
+                value = value + jnp.dot(
+                    gathered[source, span], map_ref[source], preferred_element_type=F32
+                )
+            mapped[span] = value.astype(BF16)
+
+    start_late = EARLY if relayed else 0
+    if relayed:
+        map_parts(range(CHUNKS // 2))
+
+        @pl.loop(0, batches)
+        def _(batch):
+            serve(batch, 0, EARLY, rows_dev // 2, send_early, early_copy)
+
+        rows_early[me] = send_early[me]
+        map_parts(range(CHUNKS // 2, CHUNKS))
+    else:
+        map_parts(range(CHUNKS))
 
     if relayed:
         receive_all(ask_copy)
         message = jnp.concatenate([ask_in[g] for g in range(GROUPS)], axis=0).astype(F32)
         flags = jnp.where(lane_all == LANES - 1, message, 0.0)
         flags = jnp.max(jnp.max(flags, axis=0, keepdims=True), axis=1, keepdims=True)
-        fail_ref[...] = jnp.broadcast_to(flags, (8, LANES)).astype(jnp.int32)
+        fail_ref[0, 0] = jnp.max(flags).astype(jnp.int32)
         columns = message.T.astype(jnp.int32)
         hop_iota = lax.broadcasted_iota(jnp.int32, (HOP, rows_dev), 1)
         onehot = jnp.concatenate(
@@ -319,40 +386,16 @@
         send_all(hop_copy)
         relay_rows_in[me] = relay_rows_out[me]
     else:
-        fail_ref[...] = jnp.zeros((8, LANES), jnp.int32)
-
-    batches = GROUPS // BATCH
-    lane_iota = lax.broadcasted_iota(jnp.int32, (cap, rows_dev), 1)
-
-    def serve(batch):
-        wanted = jnp.concatenate(
-            [req_in[group_at(batch + batches * item)] for item in range(BATCH)], axis=0
-        )
-        columns = wanted.astype(F32).T.astype(jnp.int32)
-        onehot = jnp.concatenate(
-            [
-                jnp.where(lane_iota == columns[:cap, item : item + 1], 1.0, 0.0).astype(BF16)
-                for item in range(BATCH)
-            ],
-            axis=0,
-        )
-        served = jnp.dot(onehot, mapped[...], preferred_element_type=F32).astype(BF16)
-        for item in range(BATCH):
-            send_rows[group_at(batch + batches * item)] = served[item * cap : (item + 1) * cap]
-        for item in range(BATCH):
-            if item:
-                row_copy(group_at(batch + batches * item), me).start()
-            else:
-
-                @pl.when(batch > 0)
-                def _():
-                    row_copy(group_at(batch), me).start()
+        fail_ref[0, 0] = 0
+
+    def serve_late(batch):
+        serve(batch, start_late, cap, rows_dev, send_rows, row_copy)
 
     early = batches // 2 if relayed else batches
 
     @pl.loop(0, early)
     def _(batch):
-        serve(batch)
+        serve_late(batch)
 
     if relayed:
         receive_all(hop_copy)
@@ -368,44 +411,88 @@
 
         @pl.loop(early, batches)
         def _(batch):
-            serve(batch)
+            serve_late(batch)
 
     rows[me] = send_rows[me]
-    receive_all(row_copy)
-    if relayed:
+    pair_tiles = LANES // cap
+
+    def pair_rows(pair):
+        pieces = []
+        for k in range(pair_tiles):
+            if relayed:
+                pieces.append(rows_early[pair * pair_tiles + k])
+            pieces.append(rows[pair * pair_tiles + k])
+        return jnp.concatenate(pieces, axis=0)
+
+    def two_tiles(first, second):
+        both = jnp.concatenate([weights[first], weights[second]], axis=1)
+        block = jnp.concatenate([pair_rows(first), pair_rows(second)], axis=0)
+        return jnp.dot(both, block, preferred_element_type=F32)
+
+    def landed_batch(batch, total):
+        for item in range(BATCH):
+            source = source_at(step_of(batch, item))
+            if relayed:
+                early_copy(source, source).wait_recv()
+            row_copy(source, source).wait_recv()
+        tile = [source_at(step_of(batch, 2 * k)) // 2 for k in range(BATCH // 2)]
+        return total + (two_tiles(tile[0], tile[1]) + two_tiles(tile[2], tile[3]))
+
+    if relayed:
+        for item in range(1, BATCH):
+            source = source_at(step_of(0, item))
+            early_copy(source, source).wait_recv()
+            row_copy(source, source).wait_recv()
+        tile = [source_at(step_of(0, 2 * k)) // 2 for k in range(BATCH // 2)]
+        first_sum = two_tiles(tile[0], tile[1]) + two_tiles(tile[2], tile[3])
+        first_sum = lax.fori_loop(1, batches, landed_batch, first_sum)
         receive_all(spill_copy)
         for g in range(GROUPS):
             spill_stage[g * SPILL : (g + 1) * SPILL] = spill_in[g].astype(F32)
 
-    def cols_copy(step, hop, target):
-        source = agree_out.at[step] if hop == 0 else agree_out.at[2 + step]
+    else:
+        receive_all(row_copy)
+
+    spans = [(low * main_tiles // 32, high * main_tiles // 32) for low, high in SPANS]
+    blocks = [(1 + low if low else 0, 1 + high) for low, high in spans]
+    blocks[-1] = (blocks[-1][0], 1 + tiles)
+
+    def cols_copy(step, hop, span, target):
+        low, high = blocks[span]
+        piece = pl.ds(low, high - low)
+        slot = (2 * step + hop) * len(blocks) + span
         return pltpu.make_async_remote_copy(
-            src_ref=source,
-            dst_ref=agree_in.at[2 * step + hop],
-            send_sem=cols_send.at[2 * step + hop],
-            recv_sem=cols_recv.at[2 * step + hop],
+            src_ref=agree_out.at[2 * hop + step, piece],
+            dst_ref=agree_in.at[2 * step + hop, piece],
+            send_sem=cols_send.at[slot],
+            recv_sem=cols_recv.at[slot],
             device_id={"cols": target},
             device_id_type=MESH,
         )
 
     lane_of = lax.broadcasted_iota(jnp.int32, (8, LANES), 1)
-    wide = 2 * LANES // cap
-
-    def landed(i):
-        return jnp.concatenate([rows[i * wide + k] for k in range(wide)], axis=0)
-
-    def weigh(i):
-        both = jnp.concatenate([weights[2 * i], weights[2 * i + 1]], axis=1)
-        return jnp.dot(both, landed(i), preferred_element_type=F32)
+
+    def forward(step, span):
+        low, high = blocks[span]
+        piece = pl.ds(low, high - low)
+        cols_copy(step, 0, span, partner).wait_recv()
+        agree_out[2 + step, piece] = agree_out[step, piece] + agree_in[2 * step, piece]
+        cols_copy(step, 1, span, cross).start()
 
     for step in range(ITERS):
-        summed = lax.fori_loop(
-            0,
-            main_tiles // 8,
-            lambda i, acc: acc
-            + ((weigh(4 * i) + weigh(4 * i + 1)) + (weigh(4 * i + 2) + weigh(4 * i + 3))),
-            jnp.zeros((pairs, half), F32),
-        )
+        if step == 0 and relayed:
+            summed = first_sum
+        else:
+            summed = lax.fori_loop(
+                0,
+                main_tiles // 8,
+                lambda i, acc: acc
+                + (
+                    (two_tiles(8 * i, 8 * i + 1) + two_tiles(8 * i + 2, 8 * i + 3))
+                    + (two_tiles(8 * i + 4, 8 * i + 5) + two_tiles(8 * i + 6, 8 * i + 7))
+                ),
+                jnp.zeros((pairs, half), F32),
+            )
         if relayed:
             spilled = spill_stage[...].astype(BF16)
             summed = summed + jnp.dot(weights[main_tiles], spilled, preferred_element_type=F32)
@@ -425,36 +512,50 @@
                     for user in range(users):
                         piece = product[user * 8 : user * 8 + 8, k * LANES : (k + 1) * LANES]
                         own = jnp.where(picked == user, piece, own)
-                    agree_out[step, tile + k] = own
-
-            @pl.loop(0, main_tiles // 4)
-            def _(i):
-                for k in range(2):
-                    agree(4 * i + 2 * k, 2, landed(2 * i + k))
-
-            if relayed:
-                agree(main_tiles, 1, spilled)
-            agree_out[step, tiles] = packed
-            cols_copy(step, 0, partner).start()
-            cols_copy(step, 0, partner).wait_recv()
-            agree_out[2 + step] = agree_out[step] + agree_in[2 * step]
-            cols_copy(step, 1, cross).start()
-            cols_copy(step, 1, cross).wait_recv()
-            squares = agree_out[2 + step, tiles] + agree_in[2 * step + 1, tiles]
-            scale = squash_scale(squares)
-            scales = [jnp.broadcast_to(scale[:, user : user + 1], (8, LANES)) for user in range(users)]
-
-            def next_weights(tile):
-                picked = users_of[tile]
-                factor = jnp.zeros((8, LANES), F32)
-                for user in range(users):
-                    factor = jnp.where(picked == user, scales[user], factor)
-                total = agree_out[2 + step, tile] + agree_in[2 * step + 1, tile]
-                value = logits[tile] + factor * total
-                logits[tile] = value
-                store_weights(tile, value)
-
-            each_tile(next_weights)
+                    agree_out[step, 1 + tile + k] = own
+
+            agree_out[step, 0] = packed
+            for span, (low, high) in enumerate(spans):
+
+                @pl.loop(low // 4, high // 4)
+                def _(i):
+                    for k in (0, 2):
+                        tile = 4 * i + k
+                        block = jnp.concatenate([pair_rows(tile), pair_rows(tile + 1)], axis=0)
+                        agree(tile, 2, block)
+
+                if relayed and high == main_tiles:
+                    agree(main_tiles, 1, spilled)
+                cols_copy(step, 0, span, partner).start()
+                if span > 0:
+                    forward(step, span - 1)
+            forward(step, len(spans) - 1)
+
+            for span, (low, high) in enumerate(spans):
+                cols_copy(step, 1, span, cross).wait_recv()
+                if span == 0:
+                    scale = squash_scale(agree_out[2 + step, 0] + agree_in[2 * step + 1, 0])
+                    scales = [
+                        jnp.broadcast_to(scale[:, user : user + 1], (8, LANES)) for user in range(users)
+                    ]
+
+                def next_weights(tile):
+                    picked = users_of[tile]
+                    factor = jnp.zeros((8, LANES), F32)
+                    for user in range(users):
+                        factor = jnp.where(picked == user, scales[user], factor)
+                    total = agree_out[2 + step, 1 + tile] + agree_in[2 * step + 1, 1 + tile]
+                    value = logits[tile] + factor * total
+                    logits[tile] = value
+                    store_weights(tile, value)
+
+                @pl.loop(low // 4, high // 4)
+                def _(i):
+                    for k in range(4):
+                        next_weights(4 * i + k)
+
+                if relayed and high == main_tiles:
+                    next_weights(main_tiles)
 
         else:
             square_out[...] = packed
@@ -494,16 +595,19 @@
             ask_copy(group_at(step), me).wait_send()
             hop_copy(group_at(step), me).wait_send()
             spill_copy(group_at(step), me).wait_send()
+            early_copy(group_at(step), me).wait_send()
 
     for step in range(ITERS - 1):
-        cols_copy(step, 0, partner).wait_send()
-        cols_copy(step, 1, cross).wait_send()
+        for span in range(len(spans)):
+            cols_copy(step, 0, span, partner).wait_send()
+            cols_copy(step, 1, span, cross).wait_send()
 
 
 def routed(cap, collective_id, item_ids, lengths, seed_rows, item_table, bilinear, seed_table):
     users, hist = item_ids.shape
     rows_dev, half = item_table.shape
-    capsules = seed_table.shape[1]
+    capsules = seed_table.shape[0]
+    late = cap - EARLY if cap < LANES else cap
     tiles = GROUPS * cap // LANES + (1 if cap < LANES else 0)
     vmem = pl.BlockSpec(memory_space=pltpu.VMEM)
     dma = pltpu.SemaphoreType.DMA
@@ -511,10 +615,10 @@
         functools.partial(kernel, cap),
         out_shape=[
             jax.ShapeDtypeStruct((users, capsules, half), F32),
-            jax.ShapeDtypeStruct((8, LANES), jnp.int32),
+            jax.ShapeDtypeStruct((1, 1), jnp.int32),
         ],
         in_specs=[vmem, pl.BlockSpec(memory_space=pltpu.SMEM), vmem, vmem, vmem, vmem],
-        out_specs=[vmem, vmem],
+        out_specs=[vmem, pl.BlockSpec(memory_space=pltpu.SMEM)],
         scratch_shapes=[
             pltpu.VMEM((GROUPS, 1, LANES), jnp.int32),
             pltpu.VMEM((GROUPS, 1, LANES), jnp.int32),
@@ -522,8 +626,10 @@
             pltpu.VMEM((tiles, 8, LANES), jnp.int32),
             pltpu.VMEM((COLS, rows_dev, half), BF16),
             pltpu.VMEM((rows_dev, half), BF16),
-            pltpu.VMEM((GROUPS, cap, half), BF16),
-            pltpu.VMEM((GROUPS, cap, half), BF16),
+            pltpu.VMEM((GROUPS, late, half), BF16),
+            pltpu.VMEM((GROUPS, late, half), BF16),
+            pltpu.VMEM((GROUPS, EARLY, half), BF16),
+            pltpu.VMEM((GROUPS, EARLY, half), BF16),
             pltpu.VMEM((tiles, 8, LANES), F32),
             pltpu.VMEM((tiles, users * capsules, LANES), BF16),
             pltpu.VMEM((4, tiles + 1, 8, LANES), F32),
@@ -541,9 +647,9 @@
             dma((GROUPS,)), dma((GROUPS,)),
             dma((2, CHUNKS)), dma((2, CHUNKS)), dma((CHUNKS,)), dma((CHUNKS,)),
             dma((GROUPS,)), dma((GROUPS,)),
-            dma((4,)), dma((4,)), dma((3,)), dma((3,)),
+            dma((4 * len(SPANS),)), dma((4 * len(SPANS),)), dma((3,)), dma((3,)),
             dma((GROUPS,)), dma((GROUPS,)), dma((GROUPS,)), dma((GROUPS,)),
-            dma((GROUPS,)), dma((GROUPS,)),
+            dma((GROUPS,)), dma((GROUPS,)), dma((GROUPS,)), dma((GROUPS,)),
         ],
         compiler_params=pltpu.CompilerParams(
             collective_id=collective_id, has_side_effects=True, vmem_limit_bytes=56 << 20
@@ -553,7 +659,7 @@
 
 def on_device(item_ids, lengths, seed_rows, item_table, bilinear, seed_table):
     maps = bilinear.reshape(COLS, -1, bilinear.shape[1])
-    args = (item_ids, lengths, seed_rows, item_table, maps, seed_table)
+    args = (item_ids, lengths, seed_rows, item_table, maps, seed_table.T)
     fast, fail = routed(64, 0, *args)
     return lax.cond(fail[0, 0] > 0, lambda: routed(LANES, 1, *args)[0], lambda: fast)
 

time: 136 us -> 122 us (0.90)
  Pallas kernels: 130 us -> 120 us
  local copies, waits for them, and re-layouts: 3.94 us -> 1.28 us
    pallas_call x1, Pallas kernels: 130 us -> 120 us  [routed(): pl.pallas_call(functools.partial(kernel, cap), out_shape=[jax.ShapeDtypeS...]
    unnamed x14 -> x13, local copies, waits for them, and re-layouts: 2.75 us -> 1.28 us
where the time goes in v3:
time: 122 us
  Pallas kernels  120 us (98%)
  local copies, waits for them, and re-layouts  1.28 us (1%)
    pallas_call x1, Pallas kernels, routed(): pl.pallas_call(functools.partial(kernel, cap), out_shape=[jax.ShapeDtypeS...  120 us

profile of v3, /device:TPU:1, one launch (start us, length us, event | category | flops | bytes accessed | tf_op | source)
XLA Modules:
  0.0 121.9 jit_solution(9622105007037059368)
XLA Ops:
  0.0 0.0 copy-start
  0.0 0.0 copy-start.1
  0.0 0.0 copy-start.2
  0.0 0.0 copy-start.3
  0.0 119.9 %shard_map.66 = (f32[16,8,256]{2,1,0:T(8,128)S(1)}, s32[1,1]{1,0:T(1,128)}) custom-call(s32[16,256]{1,0:T(8,128)} %ids_ref.1, s32[16]{0:T(128)} %len_ref.1, s32[16,256]{1,0:T(8,128)} %seed_ref.1, bf16[2048,256]{1,0:T(8,128)(2,1)} %table_ref.1, bf16[4,256,256]{2,1,0:T(8,128)(2,1)} %bitcast.3, f32[8,64]{1,0:T(8,128)} %bitcast.5), custom_call_target="tpu_custom_call" | custom-call | tf_op jit(solution)/shard_map/pallas_call | solution.py:614
  120.0 0.0 copy-start.4
  120.6 0.0 copy-start.5
  120.6 0.0 copy-done
  120.6 0.0 copy-done.1
  120.7 0.0 copy-done.2
  120.7 0.0 copy-done.3
  120.7 0.0 copy-done.4
  120.7 0.6 copy-done.5
  121.3 0.7 copy.12
  (1 shorter events, 0.0 us)
Async XLA Ops:
  0.0 120.6 %copy-start = (bf16[2048,256]{1,0:T(8,128)(2,1)S(1)}, bf16[2048,256]{1,0:T(8,128)(2,1)}, u32[]{:S(2)}) copy-start(bf16[2048,256]{1,0:T(8,128)(2,1)} %table_ref.1) | copy-start | bytes 3145732
  0.0 120.6 %copy-start.1 = (bf16[1024,256]{1,0:T(8,128)(2,1)S(1)}, bf16[1024,256]{1,0:T(8,128)(2,1)}, u32[]{:S(2)}) copy-start(bf16[1024,256]{1,0:T(8,128)(2,1)} %param.12) | copy-start | bytes 1572868
  0.0 120.7 %copy-start.2 = (s32[16,256]{1,0:T(8,128)S(1)}, s32[16,256]{1,0:T(8,128)}, u32[]{:S(2)}) copy-start(s32[16,256]{1,0:T(8,128)} %ids_ref.1) | copy-start | bytes 49156
  0.0 120.7 %copy-start.3 = (s32[16,256]{1,0:T(8,128)S(1)}, s32[16,256]{1,0:T(8,128)}, u32[]{:S(2)}) copy-start(s32[16,256]{1,0:T(8,128)} %seed_ref.1) | copy-start | bytes 49156
  120.0 0.7 copy-start.4
  120.6 0.7 copy-start.5

commit v4 on v3

--- a/solution.py
+++ b/solution.py
@@ -14,7 +14,8 @@
 BATCH = 8
 CHUNKS = 4
 HOP = 4
-EARLY = 16
+WIDE = 32
+PHASES = ((1, 8), (2, 8), (3, 16))
 SPANS = ((0, 8), (8, 16), (16, 24), (24, 32))
 SPILL = 2
 MESH = pl.DeviceIdType.MESH
@@ -42,12 +43,12 @@
     cap,
     ids_ref, len_ref, seed_ref, table_ref, map_ref, seed_table_ref,
     out_ref, fail_ref,
-    req_out, req_in, users_of, seeds_of, gathered, mapped, send_rows, rows, send_early, rows_early,
+    req_out, req_in, users_of, seeds_of, gathered, mapped, send_rows, rows,
     logits, weights, agree_out, agree_in, square_out, square_in,
     ask_out, ask_in, relay_rows_out, relay_rows_in, relay_stage, spill_out, spill_in, spill_stage,
     req_send, req_recv, tab_send, tab_recv, relay_send, relay_recv,
     row_send, row_recv, cols_send, cols_recv, sq_send, sq_recv,
-    ask_send, ask_recv, hop_send, hop_recv, spill_send, spill_recv, early_send, early_recv,
+    ask_send, ask_recv, hop_send, hop_recv, spill_send, spill_recv, early_send, early_recv, hop_onehot, *early_refs,
 ):
     me = lax.axis_index("users")
     col = lax.axis_index("cols")
@@ -64,6 +65,9 @@
     partner = col + 1 - 2 * lax.rem(col, 2)
     cross = lax.rem(col + 2, COLS)
     diagonal = lax.rem(partner + 2, COLS)
+    phases = PHASES if relayed else ()
+    early_rows = sum(size for _, size in phases)
+    early_out, early_in = early_refs[: len(phases)], early_refs[len(phases) : 2 * len(phases)]
 
     def group_at(step):
         pair = lax.rem(me // 2 + step // 2, GROUPS // 2)
@@ -89,7 +93,7 @@
     ones = jnp.ones((hist, hist), BF16)
     tri = jnp.concatenate([upper, ones], axis=0)
     before = jnp.zeros((GROUPS, hist), F32)
-    before_first = jnp.zeros((GROUPS, hist), F32)
+    before_phase = [jnp.zeros((GROUPS, hist), F32) for _ in phases]
     owners, in_rows, ranks = [], [], []
     for user in range(users):
         ids = ids_ref[user : user + 1, :]
@@ -102,16 +106,23 @@
         counts = jnp.dot(both, tri, preferred_element_type=F32)
         before = before + onehot
         rank = jnp.sum(counts * onehot, axis=0, keepdims=True) - 1.0
-        if relayed:
-            first = in_rows[user] < rows_dev // 2
-            onehot_first = jnp.where(first, onehot, 0.0)
-            both = jnp.concatenate([onehot_first.astype(BF16), before_first.astype(BF16)], axis=1)
+        free = rank + float(early_rows)
+        done, base = 0, 0
+        for k, (parts, size) in enumerate(phases):
+            low_row, high_row = done * chunk, parts * chunk
+            inside = jnp.logical_and(in_rows[user] >= low_row, in_rows[user] < high_row)
+            onehot_in = jnp.where(inside, onehot, 0.0)
+            both = jnp.concatenate([onehot_in.astype(BF16), before_phase[k].astype(BF16)], axis=1)
             counts = jnp.dot(both, tri, preferred_element_type=F32)
-            before_first = before_first + onehot_first
-            rank_first = jnp.sum(counts * onehot, axis=0, keepdims=True)
-            kept = jnp.minimum(rank_first, float(EARLY))
-            reserved = jnp.logical_and(first, rank_first <= float(EARLY))
-            rank = jnp.where(reserved, rank_first - 1.0, EARLY + rank - kept)
+            before_phase[k] = before_phase[k] + onehot_in
+            rank_in = jnp.sum(counts * onehot, axis=0, keepdims=True)
+            free = free - jnp.minimum(rank_in, float(size))
+            reserved = jnp.logical_and(inside, rank_in <= float(size))
+            rank = jnp.where(reserved, base + rank_in - 1.0, rank)
+            taken = reserved if k == 0 else jnp.logical_or(taken, reserved)
+            done, base = parts, base + size
+        if phases:
+            rank = jnp.where(taken, rank, free)
             rank = jnp.where(owner >= 0, rank, -1.0)
         ranks.append(rank.astype(jnp.int32))
     if relayed:
@@ -181,7 +192,7 @@
         return pltpu.make_async_remote_copy(
             src_ref=table_ref.at[pl.ds(part * chunk, chunk)],
             dst_ref=gathered.at[col, pl.ds(part * chunk, chunk)],
-            send_sem=tab_send.at[slot, part],
+            send_sem=tab_send.at[0],
             recv_sem=tab_recv.at[slot, part],
             device_id={"cols": target},
             device_id_type=MESH,
@@ -191,48 +202,63 @@
         return pltpu.make_async_remote_copy(
             src_ref=gathered.at[cross, pl.ds(part * chunk, chunk)],
             dst_ref=gathered.at[cross, pl.ds(part * chunk, chunk)],
-            send_sem=relay_send.at[part],
+            send_sem=tab_send.at[0],
             recv_sem=relay_recv.at[part],
             device_id={"cols": partner},
             device_id_type=MESH,
         )
 
-    def users_copy(source, landing_in, sends, recvs, target, landing):
+    def users_copy(source, landing_in, send_sem, recv_sem, target, landing):
         return pltpu.make_async_remote_copy(
             src_ref=source.at[target],
             dst_ref=landing_in.at[landing],
-            send_sem=sends.at[target],
-            recv_sem=recvs.at[landing],
+            send_sem=send_sem,
+            recv_sem=recv_sem,
             device_id={"users": target},
             device_id_type=MESH,
         )
 
-    request_copy = functools.partial(users_copy, req_out, req_in, req_send, req_recv)
-    row_copy = functools.partial(users_copy, send_rows, rows, row_send, row_recv)
-    early_copy = functools.partial(users_copy, send_early, rows_early, early_send, early_recv)
-    ask_copy = functools.partial(users_copy, ask_out, ask_in, ask_send, ask_recv)
-    hop_copy = functools.partial(users_copy, relay_rows_out, relay_rows_in, hop_send, hop_recv)
-    spill_copy = functools.partial(users_copy, spill_out, spill_in, spill_send, spill_recv)
-
-    def send_all(copy):
+    def several(source, landing_in, send_sem, recv_sem, count):
+        return pltpu.make_async_remote_copy(
+            src_ref=source.at[pl.ds(0, count)],
+            dst_ref=landing_in.at[pl.ds(0, count)],
+            send_sem=send_sem,
+            recv_sem=recv_sem,
+            device_id={"users": group_at(1)},
+            device_id_type=MESH,
+        )
+
+    request_all = (req_out, req_in, req_send.at[0], req_recv.at[0])
+    ask_all = (ask_out, ask_in, ask_send.at[0], ask_recv.at[0])
+    hop_all = (relay_rows_out, relay_rows_in, hop_send.at[0], hop_recv.at[0])
+    spill_all = (spill_out, spill_in, spill_send.at[0], spill_recv.at[0])
+    early_all = [
+        (early_out[k], early_in[k], early_send.at[k], early_recv.at[k]) for k in range(len(phases))
+    ]
+
+    def row_all(batch):
+        return (send_rows, rows, row_send.at[0], row_recv.at[batch])
+
+    def send_all(kind):
         @pl.loop(1, GROUPS)
         def _(step):
-            copy(group_at(step), me).start()
+            users_copy(*kind, group_at(step), me).start()
+
+    def receive_all(kind):
+        several(*kind, GROUPS - 1).wait_recv()
+
+    def all_left(kind):
+        several(*kind, GROUPS - 1).wait_send()
 
     def source_at(step):
         pair = lax.rem(me // 2 + GROUPS // 2 - step // 2, GROUPS // 2)
         return 2 * pair + lax.rem(me + step, 2)
 
-    def receive_all(copy):
-        @pl.loop(1, GROUPS)
-        def _(step):
-            copy(source_at(step), source_at(step)).wait_recv()
-
-    send_all(request_copy)
     for part in range(CHUNKS):
         table_copy(part, cross, 0).start()
     for part in range(CHUNKS):
         table_copy(part, partner, 1).start()
+    send_all(request_all)
     req_in[me] = req_out[me]
 
     seed_table = seed_table_ref[...]
@@ -268,7 +294,7 @@
 
     each_tile(first_weights)
 
-    receive_all(request_copy)
+    receive_all(request_all)
 
     if relayed:
         tokens = GROUPS * SPILL
@@ -302,40 +328,39 @@
             ask_out[target] = asked[target : target + 1, :]
         landed_at = jnp.where(owner >= 0, owner * HOP + rank, -1)
         landed_at = jnp.broadcast_to(landed_at, (8, tokens)).astype(F32).T.astype(jnp.int32)[:, 0:1]
-        send_all(ask_copy)
+        send_all(ask_all)
         ask_in[me] = ask_out[me]
 
     batches = GROUPS // BATCH
-    stride = 2 * batches
-
-    def step_of(batch, item):
-        return 2 * batch + stride * (item // 2) + item % 2
-
-    def serve(batch, low, high, shard, out, copy):
+
+    def step_of(batch, item, items=BATCH):
+        return 2 * batch + 2 * (GROUPS // items) * (item // 2) + item % 2
+
+    def serve(batch, items, low, high, first_row, last_row, kind):
         wanted = jnp.concatenate(
-            [req_in[group_at(step_of(batch, item))] for item in range(BATCH)], axis=0
+            [req_in[group_at(step_of(batch, item, items))] for item in range(items)], axis=0
         )
         columns = wanted.astype(F32).T.astype(jnp.int32)
-        size = high - low
-        lane_iota = lax.broadcasted_iota(jnp.int32, (size, shard), 1)
+        size, shard = high - low, last_row - first_row
+        lane_iota = lax.broadcasted_iota(jnp.int32, (size, shard), 1) + first_row
         onehot = jnp.concatenate(
             [
                 jnp.where(lane_iota == columns[low:high, item : item + 1], 1.0, 0.0).astype(BF16)
-                for item in range(BATCH)
+                for item in range(items)
             ],
             axis=0,
         )
-        served = jnp.dot(onehot, mapped[:shard], preferred_element_type=F32).astype(BF16)
-        for item in range(BATCH):
-            out[group_at(step_of(batch, item))] = served[item * size : (item + 1) * size]
-        for item in range(BATCH):
+        served = jnp.dot(onehot, mapped[first_row:last_row], preferred_element_type=F32).astype(BF16)
+        for item in range(items):
+            kind[0][group_at(step_of(batch, item, items))] = served[item * size : (item + 1) * size]
+        for item in range(items):
             if item:
-                copy(group_at(step_of(batch, item)), me).start()
+                users_copy(*kind, group_at(step_of(batch, item, items)), me).start()
             else:
 
                 @pl.when(batch > 0)
                 def _():
-                    copy(group_at(step_of(batch, 0)), me).start()
+                    users_copy(*kind, group_at(step_of(batch, 0)), me).start()
 
     def map_parts(parts):
         for part in parts:
@@ -352,44 +377,45 @@
                 )
             mapped[span] = value.astype(BF16)
 
-    start_late = EARLY if relayed else 0
-    if relayed:
-        map_parts(range(CHUNKS // 2))
-
-        @pl.loop(0, batches)
-        def _(batch):
-            serve(batch, 0, EARLY, rows_dev // 2, send_early, early_copy)
-
-        rows_early[me] = send_early[me]
-        map_parts(range(CHUNKS // 2, CHUNKS))
-    else:
-        map_parts(range(CHUNKS))
-
-    if relayed:
-        receive_all(ask_copy)
+    done, base = 0, 0
+    for k, (parts, size) in enumerate(phases):
+        map_parts(range(done, parts))
+
+        for batch in range(GROUPS // WIDE):
+            serve(batch, WIDE, base, base + size, done * chunk, parts * chunk, early_all[k])
+
+
+        early_in[k][me] = early_out[k][me]
+        done, base = parts, base + size
+    if relayed:
+        receive_all(ask_all)
         message = jnp.concatenate([ask_in[g] for g in range(GROUPS)], axis=0).astype(F32)
         flags = jnp.where(lane_all == LANES - 1, message, 0.0)
         flags = jnp.max(jnp.max(flags, axis=0, keepdims=True), axis=1, keepdims=True)
         fail_ref[0, 0] = jnp.max(flags).astype(jnp.int32)
         columns = message.T.astype(jnp.int32)
         hop_iota = lax.broadcasted_iota(jnp.int32, (HOP, rows_dev), 1)
-        onehot = jnp.concatenate(
+        hop_onehot[...] = jnp.concatenate(
             [
                 jnp.where(hop_iota == columns[:HOP, g : g + 1], 1.0, 0.0)
                 for g in range(GROUPS)
             ],
             axis=0,
         ).astype(BF16)
+    map_parts(range(done, CHUNKS))
+
+    if relayed:
+        onehot = hop_onehot[...]
         served = jnp.dot(onehot, mapped[...], preferred_element_type=F32)
         for g in range(GROUPS):
             relay_rows_out[g] = served[g * HOP : (g + 1) * HOP].astype(BF16)
-        send_all(hop_copy)
+        send_all(hop_all)
         relay_rows_in[me] = relay_rows_out[me]
     else:
         fail_ref[0, 0] = 0
 
     def serve_late(batch):
-        serve(batch, start_late, cap, rows_dev, send_rows, row_copy)
+        serve(batch, BATCH, early_rows, cap, 0, rows_dev, row_all(batch))
 
     early = batches // 2 if relayed else batches
 
@@ -398,7 +424,7 @@
         serve_late(batch)
 
     if relayed:
-        receive_all(hop_copy)
+        receive_all(hop_all)
         for g in range(GROUPS):
             relay_stage[g * HOP : (g + 1) * HOP] = relay_rows_in[g].astype(F32)
         hop_lane = lax.broadcasted_iota(jnp.int32, (tokens, GROUPS * HOP), 1)
@@ -406,7 +432,7 @@
         spilled = jnp.dot(onehot, relay_stage[...].astype(BF16), preferred_element_type=F32)
         for g in range(GROUPS):
             spill_out[g] = spilled[g * SPILL : (g + 1) * SPILL].astype(BF16)
-        send_all(spill_copy)
+        send_all(spill_all)
         spill_in[me] = spill_out[me]
 
         @pl.loop(early, batches)
@@ -419,8 +445,8 @@
     def pair_rows(pair):
         pieces = []
         for k in range(pair_tiles):
-            if relayed:
-                pieces.append(rows_early[pair * pair_tiles + k])
+            for landing_in in early_in:
+                pieces.append(landing_in[pair * pair_tiles + k])
             pieces.append(rows[pair * pair_tiles + k])
         return jnp.concatenate(pieces, axis=0)
 
@@ -429,29 +455,26 @@
         block = jnp.concatenate([pair_rows(first), pair_rows(second)], axis=0)
         return jnp.dot(both, block, preferred_element_type=F32)
 
-    def landed_batch(batch, total):
-        for item in range(BATCH):
-            source = source_at(step_of(batch, item))
-            if relayed:
-                early_copy(source, source).wait_recv()
-            row_copy(source, source).wait_recv()
+    def landed_batch(batch, total, count=BATCH):
+        several(*row_all(batch), count).wait_recv()
         tile = [source_at(step_of(batch, 2 * k)) // 2 for k in range(BATCH // 2)]
         return total + (two_tiles(tile[0], tile[1]) + two_tiles(tile[2], tile[3]))
 
     if relayed:
-        for item in range(1, BATCH):
-            source = source_at(step_of(0, item))
-            early_copy(source, source).wait_recv()
-            row_copy(source, source).wait_recv()
-        tile = [source_at(step_of(0, 2 * k)) // 2 for k in range(BATCH // 2)]
-        first_sum = two_tiles(tile[0], tile[1]) + two_tiles(tile[2], tile[3])
+        for kind in early_all:
+            receive_all(kind)
+        first_sum = landed_batch(0, jnp.zeros((pairs, half), F32), BATCH - 1)
         first_sum = lax.fori_loop(1, batches, landed_batch, first_sum)
-        receive_all(spill_copy)
+        receive_all(spill_all)
         for g in range(GROUPS):
             spill_stage[g * SPILL : (g + 1) * SPILL] = spill_in[g].astype(F32)
 
     else:
-        receive_all(row_copy)
+        several(*row_all(0), BATCH - 1).wait_recv()
+
+        @pl.loop(1, batches)
+        def _(batch):
+            several(*row_all(batch), BATCH).wait_recv()
 
     spans = [(low * main_tiles // 32, high * main_tiles // 32) for low, high in SPANS]
     blocks = [(1 + low if low else 0, 1 + high) for low, high in spans]
@@ -464,7 +487,7 @@
         return pltpu.make_async_remote_copy(
             src_ref=agree_out.at[2 * hop + step, piece],
             dst_ref=agree_in.at[2 * step + hop, piece],
-            send_sem=cols_send.at[slot],
+            send_sem=cols_send.at[0],
             recv_sem=cols_recv.at[slot],
             device_id={"cols": target},
             device_id_type=MESH,
@@ -582,32 +605,31 @@
             for copy in copies:
                 copy.wait_send()
 
-    for part in range(CHUNKS):
-        table_copy(part, cross, 0).wait_send()
-        table_copy(part, partner, 1).wait_send()
-        relay_copy(part).wait_send()
-
-    @pl.loop(1, GROUPS)
-    def _(step):
-        request_copy(group_at(step), me).wait_send()
-        row_copy(group_at(step), me).wait_send()
-        if relayed:
-            ask_copy(group_at(step), me).wait_send()
-            hop_copy(group_at(step), me).wait_send()
-            spill_copy(group_at(step), me).wait_send()
-            early_copy(group_at(step), me).wait_send()
-
-    for step in range(ITERS - 1):
-        for span in range(len(spans)):
-            cols_copy(step, 0, span, partner).wait_send()
-            cols_copy(step, 1, span, cross).wait_send()
+    def left(source, sem):
+        pltpu.make_async_remote_copy(
+            src_ref=source,
+            dst_ref=source,
+            send_sem=sem,
+            recv_sem=tab_recv.at[0, 0],
+            device_id={"cols": partner},
+            device_id_type=MESH,
+        ).wait_send()
+
+    left(gathered.at[pl.ds(0, COLS - 1)], tab_send.at[0])
+    left(agree_out, cols_send.at[0])
+    all_left(request_all)
+    all_left(row_all(0))
+    if relayed:
+        for kind in [ask_all, hop_all, spill_all] + early_all:
+            all_left(kind)
 
 
 def routed(cap, collective_id, item_ids, lengths, seed_rows, item_table, bilinear, seed_table):
     users, hist = item_ids.shape
     rows_dev, half = item_table.shape
     capsules = seed_table.shape[0]
-    late = cap - EARLY if cap < LANES else cap
+    late = cap - sum(size for _, size in PHASES) if cap < LANES else cap
+    phases = [size for _, size in PHASES]
     tiles = GROUPS * cap // LANES + (1 if cap < LANES else 0)
     vmem = pl.BlockSpec(memory_space=pltpu.VMEM)
     dma = pltpu.SemaphoreType.DMA
@@ -628,8 +650,6 @@
             pltpu.VMEM((rows_dev, half), BF16),
             pltpu.VMEM((GROUPS, late, half), BF16),
             pltpu.VMEM((GROUPS, late, half), BF16),
-            pltpu.VMEM((GROUPS, EARLY, half), BF16),
-            pltpu.VMEM((GROUPS, EARLY, half), BF16),
             pltpu.VMEM((tiles, 8, LANES), F32),
             pltpu.VMEM((tiles, users * capsules, LANES), BF16),
             pltpu.VMEM((4, tiles + 1, 8, LANES), F32),
@@ -644,12 +664,14 @@
             pltpu.VMEM((GROUPS, SPILL, half), BF16),
             pltpu.VMEM((GROUPS, SPILL, half), BF16),
             pltpu.VMEM((GROUPS * SPILL, half), F32),
-            dma((GROUPS,)), dma((GROUPS,)),
-            dma((2, CHUNKS)), dma((2, CHUNKS)), dma((CHUNKS,)), dma((CHUNKS,)),
-            dma((GROUPS,)), dma((GROUPS,)),
-            dma((4 * len(SPANS),)), dma((4 * len(SPANS),)), dma((3,)), dma((3,)),
-            dma((GROUPS,)), dma((GROUPS,)), dma((GROUPS,)), dma((GROUPS,)),
-            dma((GROUPS,)), dma((GROUPS,)), dma((GROUPS,)), dma((GROUPS,)),
+            dma((1,)), dma((1,)),
+            dma((1,)), dma((2, CHUNKS)), dma((1,)), dma((CHUNKS,)),
+            dma((1,)), dma((GROUPS // BATCH,)),
+            dma((1,)), dma((4 * len(SPANS),)), dma((3,)), dma((3,)),
+            dma((1,)), dma((1,)), dma((1,)), dma((1,)),
+            dma((1,)), dma((1,)), dma((len(PHASES),)), dma((len(PHASES),)),
+            pltpu.VMEM((GROUPS * HOP, rows_dev), BF16),
+            *[pltpu.VMEM((GROUPS, size, half), BF16) for size in phases + phases],
         ],
         compiler_params=pltpu.CompilerParams(
             collective_id=collective_id, has_side_effects=True, vmem_limit_bytes=56 << 20

time: 122 us -> 120 us (0.984)
  Pallas kernels: 120 us -> 118 us
    pallas_call x1, Pallas kernels: 120 us -> 118 us  [routed(): pl.pallas_call(functools.partial(kernel, cap), out_shape=[jax.ShapeDtypeS...]
where the time goes in v4:
time: 120 us
  Pallas kernels  118 us (98%)
  local copies, waits for them, and re-layouts  1.28 us (1%)
    pallas_call x1, Pallas kernels, routed(): pl.pallas_call(functools.partial(kernel, cap), out_shape=[jax.ShapeDtypeS...  118 us

profile of v4, /device:TPU:1, one launch (start us, length us, event | category | flops | bytes accessed | tf_op | source)
XLA Modules:
  0.0 120.2 jit_solution(2622774548287388322)
XLA Ops:
  0.0 0.0 copy-start
  0.0 0.0 copy-start.1
  0.0 0.0 copy-start.2
  0.0 0.0 copy-start.3
  0.0 118.2 %shard_map.66 = (f32[16,8,256]{2,1,0:T(8,128)S(1)}, s32[1,1]{1,0:T(1,128)}) custom-call(s32[16,256]{1,0:T(8,128)} %ids_ref.1, s32[16]{0:T(128)} %len_ref.1, s32[16,256]{1,0:T(8,128)} %seed_ref.1, bf16[2048,256]{1,0:T(8,128)(2,1)} %table_ref.1, bf16[4,256,256]{2,1,0:T(8,128)(2,1)} %bitcast.3, f32[8,64]{1,0:T(8,128)} %bitcast.5), custom_call_target="tpu_custom_call" | custom-call | tf_op jit(solution)/shard_map/pallas_call | solution.py:636
  118.2 0.0 copy-start.4
  118.9 0.0 copy-start.5
  118.9 0.0 copy-done
  118.9 0.0 copy-done.1
  118.9 0.0 copy-done.2
  118.9 0.0 copy-done.3
  118.9 0.0 copy-done.4
  118.9 0.6 copy-done.5
  119.5 0.7 copy.12
  (1 shorter events, 0.0 us)
Async XLA Ops:
  0.0 118.9 %copy-start = (bf16[2048,256]{1,0:T(8,128)(2,1)S(1)}, bf16[2048,256]{1,0:T(8,128)(2,1)}, u32[]{:S(2)}) copy-start(bf16[2048,256]{1,0:T(8,128)(2,1)} %table_ref.1) | copy-start | bytes 3145732
  0.0 118.9 %copy-start.1 = (bf16[1024,256]{1,0:T(8,128)(2,1)S(1)}, bf16[1024,256]{1,0:T(8,128)(2,1)}, u32[]{:S(2)}) copy-start(bf16[1024,256]{1,0:T(8,128)(2,1)} %param.12) | copy-start | bytes 1572868
  0.0 118.9 %copy-start.2 = (s32[16,256]{1,0:T(8,128)S(1)}, s32[16,256]{1,0:T(8,128)}, u32[]{:S(2)}) copy-start(s32[16,256]{1,0:T(8,128)} %ids_ref.1) | copy-start | bytes 49156
  0.0 118.9 %copy-start.3 = (s32[16,256]{1,0:T(8,128)S(1)}, s32[16,256]{1,0:T(8,128)}, u32[]{:S(2)}) copy-start(s32[16,256]{1,0:T(8,128)} %seed_ref.1) | copy-start | bytes 49156
  118.2 0.7 copy-start.4
  118.9 0.7 copy-start.5

commit v5 on v4

--- a/solution.py
+++ b/solution.py
@@ -254,11 +254,11 @@
         pair = lax.rem(me // 2 + GROUPS // 2 - step // 2, GROUPS // 2)
         return 2 * pair + lax.rem(me + step, 2)
 
+    send_all(request_all)
     for part in range(CHUNKS):
         table_copy(part, cross, 0).start()
     for part in range(CHUNKS):
         table_copy(part, partner, 1).start()
-    send_all(request_all)
     req_in[me] = req_out[me]
 
     seed_table = seed_table_ref[...]

time: 120 us -> 107 us (0.89)
  Pallas kernels: 118 us -> 105 us
    pallas_call x1, Pallas kernels: 118 us -> 105 us  [routed(): pl.pallas_call(functools.partial(kernel, cap), out_shape=[jax.ShapeDtypeS...]
where the time goes in v5:
time: 107 us
  Pallas kernels  105 us (98%)
  local copies, waits for them, and re-layouts  1.28 us (1%)
    pallas_call x1, Pallas kernels, routed(): pl.pallas_call(functools.partial(kernel, cap), out_shape=[jax.ShapeDtypeS...  105 us

profile of v5, /device:TPU:1, one launch (start us, length us, event | category | flops | bytes accessed | tf_op | source)
XLA Modules:
  0.0 106.5 jit_solution(13893533995938842232)
XLA Ops:
  0.0 0.0 copy-start
  0.0 0.0 copy-start.1
  0.0 0.0 copy-start.2
  0.0 0.0 copy-start.3
  0.0 104.5 %shard_map.66 = (f32[16,8,256]{2,1,0:T(8,128)S(1)}, s32[1,1]{1,0:T(1,128)}) custom-call(s32[16,256]{1,0:T(8,128)} %ids_ref.1, s32[16]{0:T(128)} %len_ref.1, s32[16,256]{1,0:T(8,128)} %seed_ref.1, bf16[2048,256]{1,0:T(8,128)(2,1)} %table_ref.1, bf16[4,256,256]{2,1,0:T(8,128)(2,1)} %bitcast.3, f32[8,64]{1,0:T(8,128)} %bitcast.5), custom_call_target="tpu_custom_call" | custom-call | tf_op jit(solution)/shard_map/pallas_call | solution.py:636
  104.6 0.0 copy-start.4
  105.2 0.0 copy-start.5
  105.2 0.0 copy-done
  105.3 0.0 copy-done.1
  105.3 0.0 copy-done.2
  105.3 0.0 copy-done.3
  105.3 0.0 copy-done.4
  105.3 0.6 copy-done.5
  105.9 0.7 copy.12
  (1 shorter events, 0.0 us)
Async XLA Ops:
  0.0 105.2 %copy-start = (bf16[2048,256]{1,0:T(8,128)(2,1)S(1)}, bf16[2048,256]{1,0:T(8,128)(2,1)}, u32[]{:S(2)}) copy-start(bf16[2048,256]{1,0:T(8,128)(2,1)} %table_ref.1) | copy-start | bytes 3145732
  0.0 105.2 %copy-start.1 = (bf16[1024,256]{1,0:T(8,128)(2,1)S(1)}, bf16[1024,256]{1,0:T(8,128)(2,1)}, u32[]{:S(2)}) copy-start(bf16[1024,256]{1,0:T(8,128)(2,1)} %param.12) | copy-start | bytes 1572868
  0.0 105.3 %copy-start.2 = (s32[16,256]{1,0:T(8,128)S(1)}, s32[16,256]{1,0:T(8,128)}, u32[]{:S(2)}) copy-start(s32[16,256]{1,0:T(8,128)} %ids_ref.1) | copy-start | bytes 49156
  0.0 105.3 %copy-start.3 = (s32[16,256]{1,0:T(8,128)S(1)}, s32[16,256]{1,0:T(8,128)}, u32[]{:S(2)}) copy-start(s32[16,256]{1,0:T(8,128)} %seed_ref.1) | copy-start | bytes 49156
  104.6 0.7 copy-start.4
  105.2 0.7 copy-start.5

commit v6 on v5

--- a/solution.py
+++ b/solution.py
@@ -15,7 +15,7 @@
 CHUNKS = 4
 HOP = 4
 WIDE = 32
-PHASES = ((1, 8), (2, 8), (3, 16))
+PHASES = ((1, 8), (2, 16), (3, 8))
 SPANS = ((0, 8), (8, 16), (16, 24), (24, 32))
 SPILL = 2
 MESH = pl.DeviceIdType.MESH

time: 107 us -> 108 us (level)
    pallas_call x1, Pallas kernels: 105 us -> 106 us  [routed(): pl.pallas_call(functools.partial(kernel, cap), out_shape=[jax.ShapeDtypeS...]
where the time goes in v6:
time: 108 us
  Pallas kernels  106 us (98%)
  local copies, waits for them, and re-layouts  1.28 us (1%)
    pallas_call x1, Pallas kernels, routed(): pl.pallas_call(functools.partial(kernel, cap), out_shape=[jax.ShapeDtypeS...  106 us

profile of v6, /device:TPU:1, one launch (start us, length us, event | category | flops | bytes accessed | tf_op | source)
XLA Modules:
  0.0 107.7 jit_solution(3675064471338085747)
XLA Ops:
  0.0 0.0 copy-start
  0.0 0.0 copy-start.1
  0.0 0.0 copy-start.2
  0.0 0.0 copy-start.3
  0.0 105.7 %shard_map.66 = (f32[16,8,256]{2,1,0:T(8,128)S(1)}, s32[1,1]{1,0:T(1,128)}) custom-call(s32[16,256]{1,0:T(8,128)} %ids_ref.1, s32[16]{0:T(128)} %len_ref.1, s32[16,256]{1,0:T(8,128)} %seed_ref.1, bf16[2048,256]{1,0:T(8,128)(2,1)} %table_ref.1, bf16[4,256,256]{2,1,0:T(8,128)(2,1)} %bitcast.3, f32[8,64]{1,0:T(8,128)} %bitcast.5), custom_call_target="tpu_custom_call" | custom-call | tf_op jit(solution)/shard_map/pallas_call | solution.py:636
  105.7 0.0 copy-start.4
  106.4 0.0 copy-start.5
  106.4 0.0 copy-done
  106.4 0.0 copy-done.1
  106.4 0.0 copy-done.2
  106.4 0.0 copy-done.3
  106.4 0.0 copy-done.4
  106.4 0.6 copy-done.5
  107.0 0.7 copy.12
  (1 shorter events, 0.0 us)
Async XLA Ops:
  0.0 106.4 %copy-start = (bf16[2048,256]{1,0:T(8,128)(2,1)S(1)}, bf16[2048,256]{1,0:T(8,128)(2,1)}, u32[]{:S(2)}) copy-start(bf16[2048,256]{1,0:T(8,128)(2,1)} %table_ref.1) | copy-start | bytes 3145732
  0.0 106.4 %copy-start.1 = (bf16[1024,256]{1,0:T(8,128)(2,1)S(1)}, bf16[1024,256]{1,0:T(8,128)(2,1)}, u32[]{:S(2)}) copy-start(bf16[1024,256]{1,0:T(8,128)(2,1)} %param.12) | copy-start | bytes 1572868
  0.0 106.4 %copy-start.2 = (s32[16,256]{1,0:T(8,128)S(1)}, s32[16,256]{1,0:T(8,128)}, u32[]{:S(2)}) copy-start(s32[16,256]{1,0:T(8,128)} %ids_ref.1) | copy-start | bytes 49156
  0.0 106.4 %copy-start.3 = (s32[16,256]{1,0:T(8,128)S(1)}, s32[16,256]{1,0:T(8,128)}, u32[]{:S(2)}) copy-start(s32[16,256]{1,0:T(8,128)} %seed_ref.1) | copy-start | bytes 49156
  105.7 0.7 copy-start.4
  106.4 0.7 copy-start.5
